TPU v7x, 512 devices: a whole 4x8x8 slice. The times are simulated.
512 devices in a mesh: img: 16 (over y, core), row: 32 (over z, x).
Axes of the slice: x: 4, y: 8, z: 8, core: 2. Of those that a mesh axis runs over, the one named last changes fastest.
Arguments:
- lat_pixels: bfloat16 [2048, 256, 320], P(('img', 'row')), parts along dimension 0, may hold values from -40 to 40
- first_gain: float32 [320], replicated, may hold values from 0.1 to 1.9
- first_beta: float32 [320], replicated, may hold values from -3 to 3
- first_kernel: bfloat16 [3, 3, 320, 320], P(None, None, 'row'), may hold values from -0.109375 to 0.109375
- time_shift: float32 [5120], P('img'), parts along dimension 0, may hold values from -3 to 3
- second_gain: float32 [320], replicated, may hold values from 0.1 to 1.9
- second_beta: float32 [320], replicated, may hold values from -3 to 3
- second_kernel: bfloat16 [3, 3, 320, 320], P(None, None, 'row'), may hold values from -0.109375 to 0.109375
- second_bias: float32 [320], replicated, may hold values from -3 to 3
Outputs:
- block_out: bfloat16 [2048, 256, 320], P(('img', 'row')), parts along dimension 0
There are 16 independent parts, one for each index of `img`. A program takes and returns all parts, laid end to end along the dimension named above; an argument that names none is the same for every part. Nothing has to cross between parts.
All inputs are finite; a program needn't handle non-finite values.
Results may differ from a plain program's by a relative error of at most 0.0024.
Values may be sent and summed in bfloat16 or wider, within the bound.
No kernel may reach another device: no remote copies, remote signals or barrier semaphores. Data moves between devices by JAX's collectives and lax.ppermute only.
A program may use at most 64 MiB of HBM per device.

v0:
```python
import jax
import jax.numpy as jnp
from jax import lax
from jax.sharding import Mesh
from jax.sharding import PartitionSpec as P

GROUPS = 32
ROW = ("row_0", "row_1")
IMG_ROW = ("img", "row_0", "row_1")


epsilon = 1e-06


def from_everyone(shard, axis):
    peers = lax.axis_size(axis)
    return lax.all_to_all(
        jnp.broadcast_to(shard[None], (peers, *shard.shape)), axis, 0, 0, tiled=True
    )


def taken_together(shard, axis):
    everything = from_everyone(shard, axis)
    return jnp.sum(everything, axis=0)


def in_one(arrays, axis):
    ends = [0]
    for a in arrays:
        ends.append(ends[-1] + a.size)
    subtotal = taken_together(jnp.concatenate([a.ravel() for a in arrays]), axis)
    return tuple((subtotal[b:e].reshape(a.shape) for a, b, e in zip(arrays, ends, ends[1:])))


def extended(cells, sides, width):
    for axis, dim in sides:
        count = lax.axis_size(axis)
        ends = count - 1
        head = lax.slice_in_dim(cells, 0, width, axis=dim)
        tail = lax.slice_in_dim(cells, cells.shape[dim] - width, cells.shape[dim], axis=dim)
        cells = jnp.concatenate(
            [
                lax.ppermute(tail, axis, [(i, (i + 1) % count) for i in range(ends)]),
                cells,
                lax.ppermute(head, axis, [((i + 1) % count, i) for i in range(ends)]),
            ],
            axis=dim,
        )
    return cells


def whole_of(shard, axes, dim):
    out = shard
    for number in range(len(axes) - 1, -1, -1):
        out = lax.all_gather(out, axes[number], axis=dim, tiled=True)
    return out


def grouped_view(pixels):
    values = pixels.astype(jnp.float32)
    channels = values.shape[-1]
    return values.reshape(-1, GROUPS, channels // GROUPS)


def normalize(pixels, center, spread, gain, beta):
    grouped = grouped_view(pixels)
    normed = (grouped - center[None, :, None]) * lax.rsqrt(spread + epsilon)[None, :, None]
    normed = normed.reshape(pixels.shape) * gain + beta
    return jax.nn.silu(normed).astype(jnp.bfloat16)


def moments(pixels):
    grouped = grouped_view(pixels)
    local_count = grouped.shape[0] * grouped.shape[2]
    totals = in_one((jnp.sum(grouped, axis=(0, 2)), jnp.sum(jnp.square(grouped), axis=(0, 2))), ROW)
    whole_count = local_count * lax.axis_size(ROW)
    center = totals[0] / whole_count
    return (center, totals[1] / whole_count - center * center)


def activated_rows(pixels, center, spread, gain, beta):
    active = normalize(pixels, center, spread, gain, beta)
    padded = extended(active, ((ROW, 0),), 1)
    return jnp.pad(padded, ((0, 0), (1, 1), (0, 0)))


def folded_conv(padded, piece):
    rows_out = padded.shape[0] - 2
    width_out = padded.shape[1] - 2
    count = piece.shape[2]
    taps = [
        padded[tap_row : tap_row + rows_out, offset : offset + width_out]
        for tap_row in range(3)
        for offset in range(3)
    ]
    columns = jnp.concatenate(taps, axis=-1).reshape(rows_out * width_out, 9 * count)
    return jnp.dot(columns, piece.reshape(9 * count, -1), preferred_element_type=jnp.float32)


def apply_kernel(padded, kernel):
    return folded_conv(padded, whole_of(kernel, ROW, 2))


def norm_conv(pixels, gain, beta, kernel):
    center, spread = moments(pixels)
    padded = activated_rows(pixels, center, spread, gain, beta)
    return apply_kernel(padded, kernel).reshape(pixels.shape)


def shards(
    lat_pixels,
    first_gain,
    first_beta,
    first_kernel,
    time_shift,
    second_gain,
    second_beta,
    second_kernel,
    second_bias,
):
    hidden = (norm_conv(lat_pixels, first_gain, first_beta, first_kernel) + time_shift).astype(
        jnp.bfloat16
    )
    hidden = lax.optimization_barrier(hidden)
    second = norm_conv(hidden, second_gain, second_beta, second_kernel)
    return (lat_pixels.astype(jnp.float32) + second + second_bias).astype(jnp.bfloat16)


def solution(mesh):
    split = Mesh(mesh.devices.reshape(mesh.shape["img"], 8, 4), ("img", "row_0", "row_1"))
    placed = (
        P(IMG_ROW, None, None),
        P(),
        P(),
        P(None, None, ROW, None),
        P("img"),
        P(),
        P(),
        P(None, None, ROW, None),
        P(),
    )
    return jax.shard_map(
        shards, mesh=split, in_specs=placed, out_specs=P(IMG_ROW, None, None), check_vma=False
    )
```

profile of v0, /device:TPU:6, one launch (start us, length us, event | category | flops | bytes accessed | tf_op | source)
XLA Modules:
  0.0 140.2 jit_solution(10656346063616102983)
XLA Ops:
  6.5 17.9 %all_gather.12 = bf16[3,3,40,320]{3,1,2,0:T(4,128)(2,1)} all-gather(bf16[3,3,10,320]{3,1,2,0:T(4,128)(2,1)} %param.12), channel_id=1, replica_groups=mesh['img'=16,'row_0'=8,'row_1'=4] {'row_1'}, dimensions={2}, use_global_device_ids=true | all-gather | bytes 288000 | tf_op jit(solution)/shard_map/all_gather | solution.py:55
  24.6 1.4 convert_reduce_fusion
  26.5 16.6 %all_to_all.12 = f32[32,1,64]{2,1,0:T(1,128)S(1)} all-to-all(f32[32,1,64]{2,1,0:T(1,128)S(1)} %broadcast_in_dim.4), channel_id=1, replica_groups=mesh['img'=16,'row_0'=8,'row_1'=4] {'row_0','row_1'}, dimensions={0} | all-to-all | bytes 16384 | tf_op jit(solution)/shard_map/all_to_all | solution.py:17
  44.2 4.0 %collective-permute-start = (bf16[1,256,320]{1,2,0:T(8,128)(2,1)S(1)}, bf16[1,256,320]{1,2,0:T(8,128)(2,1)S(1)}, u32[]{:S(2)}, u32[]{:S(2)}) collective-permute-start(bf16[1,256,320]{1,2,0:T(8,128)(2,1)S(1)} %get-tuple-element.11), channel_id=1, source_target_pairs={{0,1},{1,2},{2,3},{3,4},{4,5},{5,6},{6,7},{7,8},{8,9},{9,10},{10,1... | collective-permute-start | bytes 491528 | tf_op jit(solution)/shard_map/ppermute | solution.py:43
  48.2 1.9 %collective-permute-start.1 = (bf16[1,256,320]{1,2,0:T(8,128)(2,1)S(1)}, bf16[1,256,320]{1,2,0:T(8,128)(2,1)S(1)}, u32[]{:S(2)}, u32[]{:S(2)}) collective-permute-start(bf16[1,256,320]{1,2,0:T(8,128)(2,1)S(1)} %get-tuple-element.12), channel_id=1, source_target_pairs={{1,0},{2,1},{3,2},{4,3},{5,4},{6,5},{7,6},{8,7},{9,8},{10,9},{11,1... | collective-permute-start | bytes 491528 | tf_op jit(solution)/shard_map/ppermute | solution.py:45
  50.1 13.4 %all_gather.14 = bf16[3,3,40,320]{3,1,2,0:T(4,128)(2,1)} all-gather(bf16[3,3,10,320]{3,1,2,0:T(4,128)(2,1)S(1)} %copy-done.1), channel_id=1, replica_groups=mesh['img'=16,'row_0'=8,'row_1'=4] {'row_1'}, dimensions={2}, use_global_device_ids=true | all-gather | bytes 288000 | tf_op jit(solution)/shard_map/all_gather | solution.py:55
  64.4 0.9 slice_dynamic-update-slice_fusion.11
  65.3 0.9 fusion.32
  66.2 1.1 slice_dynamic-update-slice_fusion.10
  67.3 0.9 slice_dynamic-update-slice_fusion.9
  68.2 1.5 %constant_dynamic-update-slice_fusion = bf16[4,256,2880]{1,2,0:T(8,128)(2,1)} fusion(bf16[4,256,2880]{1,2,0:T(8,128)(2,1)} %slice_dynamic-update-slice_fusion.9, f32[320]{0:T(512)S(1)} %copy-done.2, f32[320]{0:T(512)S(1)} %copy-done.3, f32[320]{0:T(512)S(1)} %mul.57, f32[320]{0:T(512)S(1)} %sub.33, bf16[4,256,320]{1,2,0:T(8,128)(2,1)S(1)} %copy-done), kind=kLoop, calls=%fused_computation.61 | loop fusion | flops 3276800 | bytes 1315840
  69.7 1.1 slice_dynamic-update-slice_fusion.8
  70.8 0.9 slice_dynamic-update-slice_fusion.7
  71.7 0.9 fusion.31
  72.6 1.1 slice_dynamic-update-slice_fusion.6
  73.8 1.4 all-gather.3.cloned.1.call-done
  75.2 2.2 %copy.21 = bf16[3,3,320,320]{3,2,1,0:T(8,128)(2,1)S(1)} copy(bf16[3,3,320,320]{3,1,2,0:T(4,128)(2,1)} %all-gather.3.cloned.1.call-done) | data formatting | bytes 3686400 | tf_op jit(solution)/shard_map/all_gather | solution.py:55
  77.4 4.9 %fusion.7 = bf16[4,256,320]{1,2,0:T(8,128)(2,1)S(1)} fusion(bf16[4,256,2880]{1,2,0:T(8,128)(2,1)} %slice_dynamic-update-slice_fusion.6, bf16[2880,320,1]{1,0,2:T(8,128)(2,1)S(1)} %bitcast.13, f32[320]{0:T(512)S(1)} %copy-done.6), kind=kOutput, calls=%fused_computation.19 | convolution fusion | flops 1888092160 | bytes 8398080 | tf_op jit(solution)/shard_map/dot_general | solution.py:97
  83.1 15.3 %all_to_all.13 = f32[32,1,64]{2,1,0:T(1,128)S(1)} all-to-all(f32[32,1,64]{2,1,0:T(1,128)S(1)} %broadcast_in_dim.5), channel_id=1, replica_groups=mesh['img'=16,'row_0'=8,'row_1'=4] {'row_0','row_1'}, dimensions={0} | all-to-all | bytes 16384 | tf_op jit(solution)/shard_map/all_to_all | solution.py:17
  99.6 3.9 %collective-permute-start.2 = (bf16[1,256,320]{1,2,0:T(8,128)(2,1)S(1)}, bf16[1,256,320]{1,2,0:T(8,128)(2,1)S(1)}, u32[]{:S(2)}, u32[]{:S(2)}) collective-permute-start(bf16[1,256,320]{1,2,0:T(8,128)(2,1)S(1)} %get-tuple-element.9), channel_id=1, source_target_pairs={{0,1},{1,2},{2,3},{3,4},{4,5},{5,6},{6,7},{7,8},{8,9},{9,10},{10,1... | collective-permute-start | bytes 491528 | tf_op jit(solution)/shard_map/ppermute | solution.py:43
  103.5 2.1 %collective-permute-start.3 = (bf16[1,256,320]{1,2,0:T(8,128)(2,1)S(1)}, bf16[1,256,320]{1,2,0:T(8,128)(2,1)S(1)}, u32[]{:S(2)}, u32[]{:S(2)}) collective-permute-start(bf16[1,256,320]{1,2,0:T(8,128)(2,1)S(1)} %get-tuple-element.10), channel_id=1, source_target_pairs={{1,0},{2,1},{3,2},{4,3},{5,4},{6,5},{7,6},{8,7},{9,8},{10,9},{11,1... | collective-permute-start | bytes 491528 | tf_op jit(solution)/shard_map/ppermute | solution.py:45
  105.6 19.5 %all-gather.5.cloned.1.call-done = bf16[3,3,320,320]{3,1,2,0:T(4,128)(2,1)} async-done(((bf16[3,3,40,320]{3,1,2,0:T(4,128)(2,1)}), bf16[3,3,320,320]{3,1,2,0:T(4,128)(2,1)}) %all-gather.5.cloned.1.call-update) | async-done | bytes 1843216 | tf_op jit(solution)/shard_map/all_gather | solution.py:55
  125.2 2.2 %copy.24 = bf16[3,3,320,320]{3,2,1,0:T(8,128)(2,1)S(1)} copy(bf16[3,3,320,320]{3,1,2,0:T(4,128)(2,1)} %all-gather.5.cloned.1.call-done) | data formatting | bytes 3686400 | tf_op jit(solution)/shard_map/all_gather | solution.py:55
  130.3 3.1 %fusion.8 = bf16[4,256,320]{1,2,0:T(8,128)(2,1)} fusion(bf16[4,256,2880]{1,2,0:T(8,128)(2,1)S(1)} %slice_dynamic-update-slice_fusion, bf16[2880,320,1]{1,0,2:T(8,128)(2,1)S(1)} %bitcast.12, bf16[4,256,320]{1,2,0:T(8,128)(2,1)S(1)} %copy-done, f32[320]{0:T(512)S(1)} %copy-done.7), kind=kOutput, calls=%fused_computation.20 | convolution fusion | flops 1888747520 | bytes 9053440 | tf_op jit(solution)/shard_map/dot_general | solution.py:97
  (64 shorter events, 7.4 us)
Async XLA Ops:
  6.5 37.0 %copy-start = (bf16[4,256,320]{1,2,0:T(8,128)(2,1)S(1)}, bf16[4,256,320]{1,2,0:T(8,128)(2,1)}, u32[]{:S(2)}) copy-start(bf16[4,256,320]{1,2,0:T(8,128)(2,1)} %param.9) | copy-start | bytes 1966084
  6.5 37.0 %copy-start.3 = (f32[320]{0:T(512)S(1)}, f32[320]{0:T(512)}, u32[]{:S(2)}) copy-start(f32[320]{0:T(512)} %param.10) | copy-start | bytes 3844
  6.5 37.0 %copy-start.2 = (f32[320]{0:T(512)S(1)}, f32[320]{0:T(512)}, u32[]{:S(2)}) copy-start(f32[320]{0:T(512)} %param.11) | copy-start | bytes 3844
  6.5 68.6 %all-gather.3.cloned.1.call-start = ((), (), s32[]{:S(2)}) async-start(), calls=%async_computation.2 | async-start | bytes 3317760 | tf_op jit(solution)/shard_map/all_gather | solution.py:55
  24.5 25.6 %copy-start.1 = (bf16[3,3,10,320]{3,1,2,0:T(4,128)(2,1)S(1)}, bf16[3,3,10,320]{3,1,2,0:T(4,128)(2,1)}, u32[]{:S(2)}) copy-start(bf16[3,3,10,320]{3,1,2,0:T(4,128)(2,1)} %param.16) | copy-start | bytes 172804
  24.5 100.7 %all-gather.5.cloned.1.call-start = ((), (), s32[]{:S(2)}) async-start(), calls=%async_computation.3 | async-start | bytes 3317760 | tf_op jit(solution)/shard_map/all_gather | solution.py:55
  44.2 19.3 %collective-permute-start = (bf16[1,256,320]{1,2,0:T(8,128)(2,1)S(1)}, bf16[1,256,320]{1,2,0:T(8,128)(2,1)S(1)}, u32[]{:S(2)}, u32[]{:S(2)}) collective-permute-start(bf16[1,256,320]{1,2,0:T(8,128)(2,1)S(1)} %get-tuple-element.11), channel_id=1, source_target_pairs={{0,1},{1,2},{2,3},{3,4},{4,5},{5,6},{6,7},{7,8},{8,9},{9,10},{10,1... | collective-permute-start | bytes 491528 | tf_op jit(solution)/shard_map/ppermute | solution.py:43
  48.2 15.4 %collective-permute-start.1 = (bf16[1,256,320]{1,2,0:T(8,128)(2,1)S(1)}, bf16[1,256,320]{1,2,0:T(8,128)(2,1)S(1)}, u32[]{:S(2)}, u32[]{:S(2)}) collective-permute-start(bf16[1,256,320]{1,2,0:T(8,128)(2,1)S(1)} %get-tuple-element.12), channel_id=1, source_target_pairs={{1,0},{2,1},{3,2},{4,3},{5,4},{6,5},{7,6},{8,7},{9,8},{10,9},{11,1... | collective-permute-start | bytes 491528 | tf_op jit(solution)/shard_map/ppermute | solution.py:45
  73.8 3.6 %copy-start.6 = (f32[320]{0:T(512)S(1)}, f32[320]{0:T(512)}, u32[]{:S(2)}) copy-start(f32[320]{0:T(512)} %param.13) | copy-start | bytes 3844
  77.3 21.6 %copy-start.4 = (f32[320]{0:T(512)S(1)}, f32[320]{0:T(512)}, u32[]{:S(2)}) copy-start(f32[320]{0:T(512)} %param.15) | copy-start | bytes 3844
  77.4 21.6 %copy-start.5 = (f32[320]{0:T(512)S(1)}, f32[320]{0:T(512)}, u32[]{:S(2)}) copy-start(f32[320]{0:T(512)} %param.14) | copy-start | bytes 3844
  99.6 27.8 %collective-permute-start.2 = (bf16[1,256,320]{1,2,0:T(8,128)(2,1)S(1)}, bf16[1,256,320]{1,2,0:T(8,128)(2,1)S(1)}, u32[]{:S(2)}, u32[]{:S(2)}) collective-permute-start(bf16[1,256,320]{1,2,0:T(8,128)(2,1)S(1)} %get-tuple-element.9), channel_id=1, source_target_pairs={{0,1},{1,2},{2,3},{3,4},{4,5},{5,6},{6,7},{7,8},{8,9},{9,10},{10,1... | collective-permute-start | bytes 491528 | tf_op jit(solution)/shard_map/ppermute | solution.py:43
  103.5 23.8 %collective-permute-start.3 = (bf16[1,256,320]{1,2,0:T(8,128)(2,1)S(1)}, bf16[1,256,320]{1,2,0:T(8,128)(2,1)S(1)}, u32[]{:S(2)}, u32[]{:S(2)}) collective-permute-start(bf16[1,256,320]{1,2,0:T(8,128)(2,1)S(1)} %get-tuple-element.10), channel_id=1, source_target_pairs={{1,0},{2,1},{3,2},{4,3},{5,4},{6,5},{7,6},{8,7},{9,8},{10,9},{11,1... | collective-permute-start | bytes 491528 | tf_op jit(solution)/shard_map/ppermute | solution.py:45
  129.6 0.7 copy-start.7
Sparse Core Ops, SparseCore 0:
  24.6 50.4 all-gather.2
  77.2 47.8 all-gather.4
where the time goes:
time: 141 us; the launch traced here: 140 us
  blocking collectives  63.2 us (45%)
  waiting for transfers between devices  21 us (15%)
  between operations  13.7 us (10%)
  local copies, waits for them, and re-layouts  13 us (9%)
  starting transfers between devices  12 us (9%)
  other arithmetic  9.34 us (7%)
  matrix products  8.04 us (6%)
    all_to_all x2, blocking collectives, from_everyone(): lax.all_to_all(jnp.broadcast_to(shard[None], (peers, *shard.shape)), axis...  31.9 us
    all_gather x2, blocking collectives, whole_of(): out = lax.all_gather(out, axes[number], axis=dim, tiled=True)  31.3 us
    all_gather x2, waiting for transfers between devices, whole_of(): out = lax.all_gather(out, axes[number], axis=dim, tiled=True)  20.9 us
    dot_general x2, matrix products, folded_conv(): jnp.dot(columns, piece.reshape(9 * count, -1), preferred_element_type=jnp...  8.04 us
    ppermute x2, starting transfers between devices, extended(): lax.ppermute(tail, axis, [(i, (i + 1) % count) for i in range(ends)])  7.88 us
    unnamed x26, local copies, waits for them, and re-layouts  6.05 us
    all_gather x2, local copies, waits for them, and re-layouts, whole_of(): out = lax.all_gather(out, axes[number], axis=dim, tiled=True)  4.33 us
    ppermute x2, starting transfers between devices, extended(): lax.ppermute(head, axis, [((i + 1) % count, i) for i in range(ends)])  4.03 us
  transfers between devices with their start and end apart: 6, of which 2 were waited for; matrix products, arithmetic and copies ran while one was open for 17% of the time, Pallas kernels for 0%

commit v1 on v0

v1 whole, which is shorter than its diff:
```python
import functools

import jax
import jax.numpy as jnp
from jax import lax
from jax.experimental import pallas as pl
from jax.experimental.pallas import tpu as pltpu
from jax.sharding import Mesh
from jax.sharding import PartitionSpec as P

GROUPS = 32
PER = 10
CU = 320
WIDTH = 256
TAPS = 9
SLABS = TAPS * PER
PAIRS = SLABS // 2
CROWS = 23
CHUNK = 120
DEPTH = SLABS * GROUPS
ROWK = 3 * CU
ROW = ("row_0", "row_1")
IMG_ROW = ("y", "core", "row_0", "row_1")
EPS = 1e-06

f32 = jnp.float32
bf16 = jnp.bfloat16
WHOLE = pl.BlockSpec(memory_space=pltpu.VMEM)
SCALARS = pl.BlockSpec(memory_space=pltpu.SMEM)
PARAMS = pltpu.CompilerParams(vmem_limit_bytes=48 * 1024 * 1024)


def widen(ref, at, values):
    ref[at : at + CU, :] = values[:, 0:128]
    ref[at + CU : at + 2 * CU, :] = values[:, 128:256]


def slab_of(ref, j, row=0):
    at = row * 2 * CU + j
    halves = [ref[pl.ds(at + n * CU, GROUPS, stride=PER), :] for n in range(2)]
    return jnp.concatenate(halves, axis=1)


def same_slab(ref, j):
    half = ref[pl.ds(j, GROUPS, stride=PER), :]
    return jnp.concatenate([half, half], axis=1)


def local_moments(values, rows):
    total = jnp.zeros((GROUPS, WIDTH), f32)
    for h in range(rows):
        for j in range(PER):
            total += slab_of(values, j, h)
    mean = jnp.sum(total, axis=1, keepdims=True) * (1.0 / (rows * PER * WIDTH))
    off = jnp.zeros((GROUPS, WIDTH), f32)
    for h in range(rows):
        for j in range(PER):
            d = slab_of(values, j, h) - mean
            off += d * d
    return mean, jnp.sum(off, axis=1, keepdims=True)


def turned(column):
    return jnp.transpose(jnp.broadcast_to(column, (column.shape[0], 128)))


def in_three(v):
    hi = v.astype(bf16).astype(f32)
    rest = v - hi
    mid = rest.astype(bf16).astype(f32)
    return hi, mid, rest - mid


def prep_kernel(core_ref, x_ref, w_ref, ch_ref, wide, flat, chunk):
    core = core_ref[0]
    for h in range(4):
        widen(wide, h * 2 * CU, x_ref[h].astype(f32))
    fill_chunk(core, w_ref, flat, chunk)
    mean, off = local_moments(wide, 4)
    for k, col in enumerate((mean, off)):
        row = turned(col)[0:1, :]
        for n, piece in enumerate(in_three(row)):
            at = SLABS + CROWS + 3 * k + n
            chunk[at : at + 1, 0:GROUPS] = piece
    whole = chunk[...].astype(bf16)
    for d in range(GROUPS):
        ch_ref[d] = whole


def fill_chunk(core, w_ref, flat, chunk):
    for p in range(3):
        for j in range(PER):
            at = (p * PER + j) * 3
            flat[at : at + 3, 0:CU] = w_ref[p, j].astype(f32)
    chunk[...] = jnp.zeros((CHUNK, 128), f32)
    first = core == 0
    chunk[0:SLABS, :] = jnp.where(first, flat[0:SLABS, 0:128], flat[0:SLABS, 128:256])
    for c in range(2):
        t0 = (CROWS - 1) * c
        lo = flat[t0 : t0 + CROWS, 256:384]
        hi = pltpu.roll(flat[PAIRS + t0 : PAIRS + t0 + CROWS, 256:384], 64, 1)
        lane = lax.broadcasted_iota(jnp.int32, (CROWS, 128), 1)
        both = jnp.where(lane < 64, lo, hi)

        @pl.when(core == c)
        def _():
            chunk[SLABS : SLABS + CROWS, :] = both


def prep2_kernel(core_ref, w_ref, ch_ref, flat, chunk):
    fill_chunk(core_ref[0], w_ref, flat, chunk)
    whole = chunk[...].astype(bf16)
    for d in range(GROUPS):
        ch_ref[d] = whole


def prep(core, x, w):
    return pl.pallas_call(
        prep_kernel,
        out_shape=jax.ShapeDtypeStruct((GROUPS, CHUNK, 128), bf16),
        in_specs=[SCALARS, WHOLE, WHOLE],
        out_specs=WHOLE,
        scratch_shapes=[
            pltpu.VMEM((8 * CU, 128), f32),
            pltpu.VMEM((96, 384), f32),
            pltpu.VMEM((CHUNK, 128), f32),
        ],
        compiler_params=PARAMS,
        name="prep",
    )(core, x, w)


def prep2(core, w):
    return pl.pallas_call(
        prep2_kernel,
        out_shape=jax.ShapeDtypeStruct((GROUPS, CHUNK, 128), bf16),
        in_specs=[SCALARS, WHOLE],
        out_specs=WHOLE,
        scratch_shapes=[pltpu.VMEM((96, 384), f32), pltpu.VMEM((CHUNK, 128), f32)],
        compiler_params=PARAMS,
        name="prep2",
    )(core, w)


def column_of(row):
    return jnp.transpose(jnp.broadcast_to(row, (128, row.shape[1])))


def combine(means, offs, count):
    n = means.shape[0]
    center = jnp.sum(means, axis=0, keepdims=True) * (1.0 / n)
    d = means - center
    spread = (jnp.sum(offs, axis=0, keepdims=True) + count * jnp.sum(d * d, axis=0, keepdims=True)) * (
        1.0 / (n * count)
    )
    inv = lax.rsqrt(spread + EPS)
    return column_of(center), column_of(inv)


def activate(flags_ref, rows, center, inv, gain_ref, beta_ref, cols, wide, act_ref):
    gains, betas = cols
    gains[...] = column_of(gain_ref[...])
    betas[...] = column_of(beta_ref[...])
    two = lambda a: jnp.concatenate([a, a], axis=1)
    center, inv = two(center), two(inv)
    lane = lax.broadcasted_iota(jnp.int32, (GROUPS, WIDTH), 1)
    for h in range(6):
        widen(wide, 0, rows(h).astype(f32))
        for j in range(PER):
            v = (slab_of(wide, j) - center) * inv
            v = v * same_slab(gains, j) + same_slab(betas, j)
            v = v / (1.0 + jnp.exp(-v))
            if h == 0:
                v = jnp.where(flags_ref[1] == 0, 0.0, v)
            if h == 5:
                v = jnp.where(flags_ref[2] == 0, 0.0, v)
            left = jnp.where(lane == 0, 0.0, pltpu.roll(v, 1, 1))
            right = jnp.where(lane == WIDTH - 1, 0.0, pltpu.roll(v, WIDTH - 1, 1))
            at = h * ROWK + j * 3 * GROUPS
            act_ref[at : at + GROUPS, :] = left.astype(bf16)
            act_ref[at + GROUPS : at + 2 * GROUPS, :] = v.astype(bf16)
            act_ref[at + 2 * GROUPS : at + 3 * GROUPS, :] = right.astype(bf16)


def pick_rows(top_ref, mid_ref, bot_ref):
    def rows(h):
        return top_ref[0] if h == 0 else bot_ref[0] if h == 5 else mid_ref[h - 1]

    return rows


def norm1_kernel(flags_ref, g_ref, top_ref, mid_ref, bot_ref, gain_ref, beta_ref, act_ref, gains, betas, wide):
    tail = g_ref[:, CHUNK - 8 : CHUNK, :].astype(f32)
    piece = lambda n: tail[:, n, 0:GROUPS]
    means = piece(1) + piece(2) + piece(3)
    offs = piece(4) + piece(5) + piece(6)
    center, inv = combine(means, offs, 4.0 * PER * WIDTH)
    activate(flags_ref, pick_rows(top_ref, mid_ref, bot_ref), center, inv, gain_ref, beta_ref, (gains, betas), wide, act_ref)


def norm2_kernel(flags_ref, s_ref, top_ref, mid_ref, bot_ref, gain_ref, beta_ref, act_ref, gains, betas, wide):
    both = s_ref[:, 0, :]
    center, inv = combine(both[:, 0:GROUPS], both[:, GROUPS : 2 * GROUPS], 4.0 * PER * WIDTH)
    activate(flags_ref, pick_rows(top_ref, mid_ref, bot_ref), center, inv, gain_ref, beta_ref, (gains, betas), wide, act_ref)


def norm(kernel, flags, stats, top, mid, bot, gain, beta):
    return pl.pallas_call(
        kernel,
        out_shape=jax.ShapeDtypeStruct((6 * ROWK, WIDTH), bf16),
        in_specs=[SCALARS] + [WHOLE] * 6,
        out_specs=WHOLE,
        scratch_shapes=[pltpu.VMEM((CU, 128), f32), pltpu.VMEM((CU, 128), f32), pltpu.VMEM((2 * CU, 128), f32)],
        compiler_params=PARAMS,
        name=kernel.__name__,
    )(flags, stats, top, mid, bot, gain.reshape(1, CU), beta.reshape(1, CU))


def gather_half(core, g_ref, wide, w):
    for d in range(GROUPS):
        wide[d * CHUNK : (d + 1) * CHUNK, :] = g_ref[d].astype(f32)
    lanes = pl.ds(pl.multiple_of(core * 128, 128), 128)
    for m in range(SLABS):
        v = wide[pl.ds(m, GROUPS, stride=CHUNK), :]
        w[m * GROUPS : (m + 1) * GROUPS, lanes] = v.astype(bf16)
    t0 = core * (CROWS - 1)
    for t in range(CROWS):
        v = wide[pl.ds(SLABS + t, GROUPS, stride=CHUNK), :]
        at = pl.multiple_of((t0 + t) * GROUPS, GROUPS)
        w[pl.ds(at, GROUPS), 256:384] = v.astype(bf16)
        w[pl.ds(at + PAIRS * GROUPS, GROUPS), 256:384] = pltpu.roll(v, 64, 1).astype(bf16)


def weights(flags_ref, own_ref, other_ref, wide, w, wt):
    core = flags_ref[0]
    gather_half(core, own_ref, wide, w)
    gather_half(1 - core, other_ref, wide, w)
    for p in range(3):
        wt[p] = jnp.transpose(w[p * ROWK : (p + 1) * ROWK, 0:CU])


def conv_row(h, act_ref, wt):
    total = None
    for p in range(3):
        part = jnp.dot(
            wt[p], act_ref[(h + p) * ROWK : (h + p + 1) * ROWK, :], preferred_element_type=f32
        )
        total = part if total is None else total + part
    return total


def conv1_kernel(flags_ref, own_ref, other_ref, act_ref, shift_ref, hid_ref, st_ref, wide, w, wt, full):
    weights(flags_ref, own_ref, other_ref, wide, w, wt)
    shift = column_of(shift_ref[...])
    shift = jnp.concatenate([shift, shift], axis=1)
    for h in range(4):
        row = (conv_row(h, act_ref, wt) + shift).astype(bf16)
        hid_ref[h] = row
        widen(full, h * 2 * CU, row.astype(f32))
    mean, off = local_moments(full, 4)
    line = turned(jnp.concatenate([mean, off], axis=0))[0:1, :]
    line = jnp.concatenate([line, jnp.zeros((1, 64), f32)], axis=1)
    for d in range(GROUPS):
        st_ref[d] = line


CONV_SCRATCH = [
    pltpu.VMEM((GROUPS * CHUNK, 128), f32),
    pltpu.VMEM((DEPTH, 384), bf16),
    pltpu.VMEM((3, CU, ROWK), bf16),
]


def conv1(flags, own, other, act, shift):
    return pl.pallas_call(
        conv1_kernel,
        out_shape=(
            jax.ShapeDtypeStruct((4, CU, WIDTH), bf16),
            jax.ShapeDtypeStruct((GROUPS, 1, 128), f32),
        ),
        in_specs=[SCALARS] + [WHOLE] * 4,
        out_specs=(WHOLE, WHOLE),
        scratch_shapes=CONV_SCRATCH + [pltpu.VMEM((8 * CU, 128), f32)],
        compiler_params=PARAMS,
        name="conv1",
    )(flags, own, other, act, shift.reshape(1, CU))


def conv2_kernel(flags_ref, own_ref, other_ref, act_ref, bias_ref, x_ref, out_ref, wide, w, wt):
    weights(flags_ref, own_ref, other_ref, wide, w, wt)
    bias = column_of(bias_ref[...])
    bias = jnp.concatenate([bias, bias], axis=1)
    for h in range(4):
        out_ref[h] = (x_ref[h].astype(f32) + conv_row(h, act_ref, wt) + bias).astype(bf16)


def conv2(flags, own, other, act, bias, x):
    return pl.pallas_call(
        conv2_kernel,
        out_shape=jax.ShapeDtypeStruct((4, CU, WIDTH), bf16),
        in_specs=[SCALARS] + [WHOLE] * 5,
        out_specs=WHOLE,
        scratch_shapes=CONV_SCRATCH,
        compiler_params=PARAMS,
        name="conv2",
    )(flags, own, other, act, bias.reshape(1, CU), x)


def to_all(chunks):
    return lax.all_to_all(chunks, ROW, 0, 0, tiled=True)


def swapped(chunks):
    return lax.ppermute(chunks, "core", [(0, 1), (1, 0)])


def edges(rows):
    count = lax.axis_size(ROW)
    above = lax.ppermute(rows[3:4], ROW, [(i, i + 1) for i in range(count - 1)])
    below = lax.ppermute(rows[0:1], ROW, [(i + 1, i) for i in range(count - 1)])
    return above, below


def shards(
    lat_pixels,
    first_gain,
    first_beta,
    first_kernel,
    time_shift,
    second_gain,
    second_beta,
    second_kernel,
    second_bias,
):
    x = lat_pixels.transpose(0, 2, 1)
    place = lax.axis_index(ROW)
    last = lax.axis_size(ROW) - 1
    flags = jnp.stack(
        [lax.axis_index("core"), (place > 0).astype(jnp.int32), (place < last).astype(jnp.int32)]
    ).astype(jnp.int32)
    ch1 = prep(flags, x, first_kernel.transpose(0, 2, 1, 3))
    ch2 = prep2(flags, second_kernel.transpose(0, 2, 1, 3))
    own1 = to_all(ch1)
    own2 = to_all(ch2)
    above, below = edges(x)
    other1 = swapped(own1)
    act = norm(norm1_kernel, flags, own1, above, x, below, first_gain, first_beta)
    hidden, st = conv1(flags, own1, other1, act, time_shift)
    habove, hbelow = edges(hidden)
    stats = to_all(st)
    other2 = swapped(own2)
    act2 = norm(norm2_kernel, flags, stats, habove, hidden, hbelow, second_gain, second_beta)
    out = conv2(flags, own2, other2, act2, second_bias, x)
    return out.transpose(0, 2, 1)


def solution(mesh):
    split = Mesh(mesh.devices.reshape(mesh.shape["img"] // 2, 2, 8, 4), ("y", "core", "row_0", "row_1"))
    placed = (
        P(IMG_ROW, None, None),
        P(),
        P(),
        P(None, None, ROW, None),
        P(("y", "core")),
        P(),
        P(),
        P(None, None, ROW, None),
        P(),
    )
    return jax.shard_map(
        shards, mesh=split, in_specs=placed, out_specs=P(IMG_ROW, None, None), check_vma=False
    )
```

time: 141 us -> 130 us (0.922); the launches traced: 140 us -> 128 us
  blocking collectives: 63.2 us -> 0 us
  waiting for transfers between devices: 21 us -> 63.9 us
  starting transfers between devices: 12 us -> 42.5 us
  Pallas kernels: 0 us -> 17.9 us
  between operations: 13.7 us -> 0.27 us
  local copies, waits for them, and re-layouts: 13 us -> 3.04 us
  other arithmetic: 9.34 us -> 0.08 us
  matrix products: 8.04 us -> 0 us
    all_to_all x0 -> x3, waiting for transfers between devices: none -> 56.5 us  [to_all(): return lax.all_to_all(chunks, ROW, 0, 0, tiled=True)]
    all_to_all x2 -> x0, blocking collectives: 31.9 us -> none  [from_everyone(): lax.all_to_all(jnp.broadcast_to(shard[None], (peers, *shard.shape)), axis...]
    all_gather x2 -> x0, blocking collectives: 31.3 us -> none  [whole_of(): out = lax.all_gather(out, axes[number], axis=dim, tiled=True)]
    all_to_all x0 -> x3, starting transfers between devices: none -> 27 us  [to_all(): return lax.all_to_all(chunks, ROW, 0, 0, tiled=True)]
    all_gather x2 -> x0, waiting for transfers between devices: 20.9 us -> none  [whole_of(): out = lax.all_gather(out, axes[number], axis=dim, tiled=True)]
    pallas_call x0 -> x6, Pallas kernels: none -> 17.9 us  [the longest x1 5.55 us: conv1(): pl.pallas_call(conv1_kernel, out_shape=(jax.ShapeDtypeStruct((4, CU, WIDT...]
    dot_general x2 -> x0, matrix products: 8.04 us -> none  [folded_conv(): jnp.dot(columns, piece.reshape(9 * count, -1), preferred_element_type=jnp...]
    ppermute x4 -> x6, waiting for transfers between devices: 0.01 us -> 7.39 us  [the longest x2 4.81 us: edges(): below = lax.ppermute(rows[0:1], ROW, [(i + 1, i) for i in range(count - 1)])]
  transfers between devices with their start and end apart: 6 -> 9, of which waited for: 2 -> 5; matrix products, arithmetic and copies ran while one was open for 17% -> 0% of each run, Pallas kernels for 0% -> 8%
where the time goes in v1:
time: 130 us; the launch traced here: 128 us
  waiting for transfers between devices  63.9 us (49%)
  starting transfers between devices  42.5 us (33%)
  Pallas kernels  17.9 us (14%)
  local copies, waits for them, and re-layouts  3.04 us (2%)
    all_to_all x3, waiting for transfers between devices, to_all(): return lax.all_to_all(chunks, ROW, 0, 0, tiled=True)  56.5 us
    all_to_all x3, starting transfers between devices, to_all(): return lax.all_to_all(chunks, ROW, 0, 0, tiled=True)  27 us
    ppermute x2, starting transfers between devices, edges(): below = lax.ppermute(rows[0:1], ROW, [(i + 1, i) for i in range(count - 1)])  6.8 us
    pallas_call x1, Pallas kernels, conv1(): pl.pallas_call(conv1_kernel, out_shape=(jax.ShapeDtypeStruct((4, CU, WIDT...  5.55 us
    pallas_call x1, Pallas kernels, conv2(): pl.pallas_call(conv2_kernel, out_shape=jax.ShapeDtypeStruct((4, CU, WIDTH...  5.34 us
    ppermute x2, starting transfers between devices, edges(): above = lax.ppermute(rows[3:4], ROW, [(i, i + 1) for i in range(count - 1)])  4.89 us
    ppermute x2, waiting for transfers between devices, edges(): below = lax.ppermute(rows[0:1], ROW, [(i + 1, i) for i in range(count - 1)])  4.81 us
    pallas_call x2, Pallas kernels, norm(): pl.pallas_call(kernel, out_shape=jax.ShapeDtypeStruct((6 * ROWK, WIDTH),...  4.13 us
  transfers between devices with their start and end apart: 9, of which 5 were waited for; matrix products, arithmetic and copies ran while one was open for 0% of the time, Pallas kernels for 8%

profile of v1, /device:TPU:6, one launch (start us, length us, event | category | flops | bytes accessed | tf_op | source)
XLA Modules:
  0.0 127.7 jit_solution(884134075242036217)
XLA Ops:
  0.0 0.1 pad_add_fusion.core_ref.flags_ref
  0.1 1.1 copy-done
  1.2 0.9 copy-done.3
  2.1 2.1 %prep.1 = bf16[32,120,128]{2,1,0:T(8,128)(2,1)} custom-call(s32[3]{0:T(128)S(1)} %pad_add_fusion.core_ref.flags_ref, bf16[4,320,256]{2,1,0:T(8,128)(2,1)S(1)} %bitcast.7, bf16[3,10,3,320]{3,2,1,0:T(4,128)(2,1)S(1)} %bitcast.11), custom_call_target="tpu_custom_call" | custom-call | tf_op jit(solution)/shard_map/prep/pallas_call | solution.py:118
  4.2 13.5 %all-to-all-start.1 = ((bf16[32,120,128]{2,1,0:T(8,128)(2,1)}), bf16[32,120,128]{2,1,0:T(8,128)(2,1)S(1)}, u32[]{:S(2)}, u32[]{:S(2)}) async-start(bf16[32,120,128]{2,1,0:T(8,128)(2,1)} %prep.1), calls=%async_computation.1 | async-start | bytes 1966080 | tf_op jit(solution)/shard_map/all_to_all | solution.py:310
  17.8 0.8 prep2.1
  18.5 1.0 copy-done.2
  19.5 24.9 %all-to-all-done.1.g_ref.own_ref = bf16[32,120,128]{2,1,0:T(8,128)(2,1)S(1)} async-done(((bf16[32,120,128]{2,1,0:T(8,128)(2,1)}), bf16[32,120,128]{2,1,0:T(8,128)(2,1)S(1)}, u32[]{:S(2)}, u32[]{:S(2)}) %all-to-all-start.1) | async-done | bytes 983072 | tf_op jit(solution)/shard_map/all_to_all | solution.py:310
  44.4 5.6 %all-to-all-start = ((bf16[32,120,128]{2,1,0:T(8,128)(2,1)}), bf16[32,120,128]{2,1,0:T(8,128)(2,1)S(1)}, u32[]{:S(2)}, u32[]{:S(2)}) async-start(bf16[32,120,128]{2,1,0:T(8,128)(2,1)} %copy-done.2), calls=%async_computation | async-start | bytes 1966080 | tf_op jit(solution)/shard_map/all_to_all | solution.py:310
  50.0 1.9 %collective-permute-start.1 = (bf16[32,120,128]{2,1,0:T(8,128)(2,1)S(1)}, bf16[32,120,128]{2,1,0:T(8,128)(2,1)}, u32[]{:S(2)}, u32[]{:S(2)}) collective-permute-start(bf16[32,120,128]{2,1,0:T(8,128)(2,1)S(1)} %all-to-all-done.1.g_ref.own_ref), channel_id=1, source_target_pairs={{0,32},{32,0},{1,33},{33,1},{2,34},{34,2},{3,35},{35,3},{4,36},{36... | collective-permute-start | bytes 2949128 | tf_op jit(solution)/shard_map/ppermute | solution.py:314
  51.9 23.7 %all-to-all-done.own_ref = bf16[32,120,128]{2,1,0:T(8,128)(2,1)S(1)} async-done(((bf16[32,120,128]{2,1,0:T(8,128)(2,1)}), bf16[32,120,128]{2,1,0:T(8,128)(2,1)S(1)}, u32[]{:S(2)}, u32[]{:S(2)}) %all-to-all-start) | async-done | bytes 983072 | tf_op jit(solution)/shard_map/all_to_all | solution.py:310
  75.6 1.9 %collective-permute-start = (bf16[32,120,128]{2,1,0:T(8,128)(2,1)S(1)}, bf16[32,120,128]{2,1,0:T(8,128)(2,1)}, u32[]{:S(2)}, u32[]{:S(2)}) collective-permute-start(bf16[32,120,128]{2,1,0:T(8,128)(2,1)S(1)} %all-to-all-done.own_ref), channel_id=1, source_target_pairs={{0,32},{32,0},{1,33},{33,1},{2,34},{34,2},{3,35},{35,3},{4,36},{36... | collective-permute-start | bytes 2949128 | tf_op jit(solution)/shard_map/ppermute | solution.py:314
  77.6 3.0 %collective-permute-start.2 = (bf16[1,320,256]{2,1,0:T(8,128)(2,1)S(1)}, bf16[1,320,256]{2,1,0:T(8,128)(2,1)S(1)}, u32[]{:S(2)}, u32[]{:S(2)}) collective-permute-start(bf16[1,320,256]{2,1,0:T(8,128)(2,1)S(1)} %get-tuple-element.12), channel_id=1, source_target_pairs={{0,1},{1,2},{2,3},{3,4},{4,5},{5,6},{6,7},{7,8},{8,9},{9,10},{10,1... | collective-permute-start | bytes 491528 | tf_op jit(solution)/shard_map/ppermute | solution.py:319
  80.6 2.9 %collective-permute-start.3 = (bf16[1,320,256]{2,1,0:T(8,128)(2,1)S(1)}, bf16[1,320,256]{2,1,0:T(8,128)(2,1)S(1)}, u32[]{:S(2)}, u32[]{:S(2)}) collective-permute-start(bf16[1,320,256]{2,1,0:T(8,128)(2,1)S(1)} %get-tuple-element.11), channel_id=1, source_target_pairs={{1,0},{2,1},{3,2},{4,3},{5,4},{6,5},{7,6},{8,7},{9,8},{10,9},{11,1... | collective-permute-start | bytes 491528 | tf_op jit(solution)/shard_map/ppermute | solution.py:320
  83.5 2.6 %collective-permute-done.2.top_ref = bf16[1,320,256]{2,1,0:T(8,128)(2,1)S(1)} collective-permute-done((bf16[1,320,256]{2,1,0:T(8,128)(2,1)S(1)}, bf16[1,320,256]{2,1,0:T(8,128)(2,1)S(1)}, u32[]{:S(2)}, u32[]{:S(2)}) %collective-permute-start.2) | collective-permute-done | bytes 163872 | tf_op jit(solution)/shard_map/ppermute | solution.py:319
  86.1 4.8 %collective-permute-done.3.bot_ref = bf16[1,320,256]{2,1,0:T(8,128)(2,1)S(1)} collective-permute-done((bf16[1,320,256]{2,1,0:T(8,128)(2,1)S(1)}, bf16[1,320,256]{2,1,0:T(8,128)(2,1)S(1)}, u32[]{:S(2)}, u32[]{:S(2)}) %collective-permute-start.3) | collective-permute-done | bytes 163872 | tf_op jit(solution)/shard_map/ppermute | solution.py:320
  90.9 2.0 %norm1_kernel.1.act_ref = bf16[5760,256]{1,0:T(8,128)(2,1)S(1)} custom-call(s32[3]{0:T(128)S(1)} %pad_add_fusion.core_ref.flags_ref, bf16[32,120,128]{2,1,0:T(8,128)(2,1)S(1)} %all-to-all-done.1.g_ref.own_ref, bf16[1,320,256]{2,1,0:T(8,128)(2,1)S(1)} %collective-permute-done.2.top_ref, bf16[4,320,256]{2,1,0:T(8,128)(2,1)S(1)} %bitcast.9, ...), custom_call_target="tpu_custom_call" | custom-call | tf_op jit(solution)/shard_map/norm1_kernel/pallas_call | solution.py:208
  92.9 5.6 %conv1.1 = (bf16[4,320,256]{2,1,0:T(8,128)(2,1)S(1)}, f32[32,1,128]{2,1,0:T(1,128)}) custom-call(s32[3]{0:T(128)S(1)} %pad_add_fusion.core_ref.flags_ref, bf16[32,120,128]{2,1,0:T(8,128)(2,1)S(1)} %all-to-all-done.1.g_ref.own_ref, bf16[32,120,128]{2,1,0:T(8,128)(2,1)} %collective-permute-done.1.other_ref, bf16[5760,256]{1,0:T(8,128)(2,1)S(1)} %norm1_kernel.1.act_ref, ...), custom_call_target="tpu_custom_call" | custom-call | tf_op jit(solution)/shard_map/conv1/pallas_call | solution.py:275
  98.5 1.9 %collective-permute-start.4 = (bf16[1,320,256]{2,1,0:T(8,128)(2,1)S(1)}, bf16[1,320,256]{2,1,0:T(8,128)(2,1)S(1)}, u32[]{:S(2)}, u32[]{:S(2)}) collective-permute-start(bf16[1,320,256]{2,1,0:T(8,128)(2,1)S(1)} %get-tuple-element.10), channel_id=1, source_target_pairs={{0,1},{1,2},{2,3},{3,4},{4,5},{5,6},{6,7},{7,8},{8,9},{9,10},{10,1... | collective-permute-start | bytes 491528 | tf_op jit(solution)/shard_map/ppermute | solution.py:319
  100.4 3.9 %collective-permute-start.5 = (bf16[1,320,256]{2,1,0:T(8,128)(2,1)S(1)}, bf16[1,320,256]{2,1,0:T(8,128)(2,1)S(1)}, u32[]{:S(2)}, u32[]{:S(2)}) collective-permute-start(bf16[1,320,256]{2,1,0:T(8,128)(2,1)S(1)} %get-tuple-element.9), channel_id=1, source_target_pairs={{1,0},{2,1},{3,2},{4,3},{5,4},{6,5},{7,6},{8,7},{9,8},{10,9},{11,1... | collective-permute-start | bytes 491528 | tf_op jit(solution)/shard_map/ppermute | solution.py:320
  104.4 7.9 %all-to-all-start.2 = ((f32[32,1,128]{2,1,0:T(1,128)}), f32[32,1,128]{2,1,0:T(1,128)S(1)}, u32[]{:S(2)}, u32[]{:S(2)}) async-start(f32[32,1,128]{2,1,0:T(1,128)} %get-tuple-element.7), calls=%async_computation.2 | async-start | bytes 32768 | tf_op jit(solution)/shard_map/all_to_all | solution.py:310
  112.3 7.8 %all-to-all-done.2.s_ref = f32[32,1,128]{2,1,0:T(1,128)S(1)} async-done(((f32[32,1,128]{2,1,0:T(1,128)}), f32[32,1,128]{2,1,0:T(1,128)S(1)}, u32[]{:S(2)}, u32[]{:S(2)}) %all-to-all-start.2) | async-done | bytes 16416 | tf_op jit(solution)/shard_map/all_to_all | solution.py:310
  120.2 2.2 %norm2_kernel.1.act_ref = bf16[5760,256]{1,0:T(8,128)(2,1)S(1)} custom-call(s32[3]{0:T(128)S(1)} %pad_add_fusion.core_ref.flags_ref, f32[32,1,128]{2,1,0:T(1,128)S(1)} %all-to-all-done.2.s_ref, bf16[1,320,256]{2,1,0:T(8,128)(2,1)S(1)} %collective-permute-done.4.top_ref, bf16[4,320,256]{2,1,0:T(8,128)(2,1)S(1)} %get-tuple-element.8.mid_ref, ...), custom_call_target="tpu_custom_call" | custom-call | tf_op jit(solution)/shard_map/norm2_kernel/pallas_call | solution.py:208
  122.4 5.3 %conv2.1 = bf16[4,320,256]{2,1,0:T(8,128)(2,1)} custom-call(s32[3]{0:T(128)S(1)} %pad_add_fusion.core_ref.flags_ref, bf16[32,120,128]{2,1,0:T(8,128)(2,1)S(1)} %all-to-all-done.own_ref, bf16[32,120,128]{2,1,0:T(8,128)(2,1)} %collective-permute-done.other_ref, bf16[5760,256]{1,0:T(8,128)(2,1)S(1)} %norm2_kernel.1.act_ref, f32[1,320]{1,0:T(1,128)S(1)} %reshape.23.bias_ref, ...), custom_call_target="tpu_custom_call" | custom-call | tf_op jit(solution)/shard_map/conv2/pallas_call | solution.py:298
  (31 shorter events, 0.1 us)
Async XLA Ops:
  0.1 1.1 copy-start
  1.2 0.9 copy-start.3
  2.1 15.7 %copy-start.4 = (bf16[3,3,10,320]{3,1,2,0:T(4,128)(2,1)S(1)}, bf16[3,3,10,320]{3,1,2,0:T(4,128)(2,1)}, u32[]{:S(2)}) copy-start(bf16[3,3,10,320]{3,1,2,0:T(4,128)(2,1)} %param.16) | copy-start | bytes 172804
  2.1 75.5 %copy-start.1 = (bf16[4,256,320]{1,2,0:T(8,128)(2,1)S(1)}, bf16[4,256,320]{1,2,0:T(8,128)(2,1)}, u32[]{:S(2)}) copy-start(bf16[4,256,320]{1,2,0:T(8,128)(2,1)} %param.9) | copy-start | bytes 1966084
  4.2 79.3 %copy-start.5 = (f32[320]{0:T(512)S(1)}, f32[320]{0:T(512)}, u32[]{:S(2)}) copy-start(f32[320]{0:T(512)} %param.10) | copy-start | bytes 3844
  4.2 79.3 %copy-start.6 = (f32[320]{0:T(512)S(1)}, f32[320]{0:T(512)}, u32[]{:S(2)}) copy-start(f32[320]{0:T(512)} %param.11) | copy-start | bytes 3844
  4.2 79.3 %copy-start.7 = (f32[320]{0:T(512)S(1)}, f32[320]{0:T(512)}, u32[]{:S(2)}) copy-start(f32[320]{0:T(512)} %param.13) | copy-start | bytes 3844
  4.2 40.2 %all-to-all-start.1 = ((bf16[32,120,128]{2,1,0:T(8,128)(2,1)}), bf16[32,120,128]{2,1,0:T(8,128)(2,1)S(1)}, u32[]{:S(2)}, u32[]{:S(2)}) async-start(bf16[32,120,128]{2,1,0:T(8,128)(2,1)} %prep.1), calls=%async_computation.1 | async-start | bytes 1966080 | tf_op jit(solution)/shard_map/all_to_all | solution.py:310
  18.5 1.0 copy-start.2
  44.4 31.2 %all-to-all-start = ((bf16[32,120,128]{2,1,0:T(8,128)(2,1)}), bf16[32,120,128]{2,1,0:T(8,128)(2,1)S(1)}, u32[]{:S(2)}, u32[]{:S(2)}) async-start(bf16[32,120,128]{2,1,0:T(8,128)(2,1)} %copy-done.2), calls=%async_computation | async-start | bytes 1966080 | tf_op jit(solution)/shard_map/all_to_all | solution.py:310
  50.0 42.9 %collective-permute-start.1 = (bf16[32,120,128]{2,1,0:T(8,128)(2,1)S(1)}, bf16[32,120,128]{2,1,0:T(8,128)(2,1)}, u32[]{:S(2)}, u32[]{:S(2)}) collective-permute-start(bf16[32,120,128]{2,1,0:T(8,128)(2,1)S(1)} %all-to-all-done.1.g_ref.own_ref), channel_id=1, source_target_pairs={{0,32},{32,0},{1,33},{33,1},{2,34},{34,2},{3,35},{35,3},{4,36},{36... | collective-permute-start | bytes 2949128 | tf_op jit(solution)/shard_map/ppermute | solution.py:314
  75.6 46.7 %collective-permute-start = (bf16[32,120,128]{2,1,0:T(8,128)(2,1)S(1)}, bf16[32,120,128]{2,1,0:T(8,128)(2,1)}, u32[]{:S(2)}, u32[]{:S(2)}) collective-permute-start(bf16[32,120,128]{2,1,0:T(8,128)(2,1)S(1)} %all-to-all-done.own_ref), channel_id=1, source_target_pairs={{0,32},{32,0},{1,33},{33,1},{2,34},{34,2},{3,35},{35,3},{4,36},{36... | collective-permute-start | bytes 2949128 | tf_op jit(solution)/shard_map/ppermute | solution.py:314
  77.6 8.5 %collective-permute-start.2 = (bf16[1,320,256]{2,1,0:T(8,128)(2,1)S(1)}, bf16[1,320,256]{2,1,0:T(8,128)(2,1)S(1)}, u32[]{:S(2)}, u32[]{:S(2)}) collective-permute-start(bf16[1,320,256]{2,1,0:T(8,128)(2,1)S(1)} %get-tuple-element.12), channel_id=1, source_target_pairs={{0,1},{1,2},{2,3},{3,4},{4,5},{5,6},{6,7},{7,8},{8,9},{9,10},{10,1... | collective-permute-start | bytes 491528 | tf_op jit(solution)/shard_map/ppermute | solution.py:319
  80.6 10.3 %collective-permute-start.3 = (bf16[1,320,256]{2,1,0:T(8,128)(2,1)S(1)}, bf16[1,320,256]{2,1,0:T(8,128)(2,1)S(1)}, u32[]{:S(2)}, u32[]{:S(2)}) collective-permute-start(bf16[1,320,256]{2,1,0:T(8,128)(2,1)S(1)} %get-tuple-element.11), channel_id=1, source_target_pairs={{1,0},{2,1},{3,2},{4,3},{5,4},{6,5},{7,6},{8,7},{9,8},{10,9},{11,1... | collective-permute-start | bytes 491528 | tf_op jit(solution)/shard_map/ppermute | solution.py:320
  92.9 19.4 %copy-start.8 = (f32[320]{0:T(512)S(1)}, f32[320]{0:T(512)}, u32[]{:S(2)}) copy-start(f32[320]{0:T(512)} %param.14) | copy-start | bytes 3844
  92.9 19.4 %copy-start.9 = (f32[320]{0:T(512)S(1)}, f32[320]{0:T(512)}, u32[]{:S(2)}) copy-start(f32[320]{0:T(512)} %param.15) | copy-start | bytes 3844
  92.9 19.4 %copy-start.10 = (f32[320]{0:T(512)S(1)}, f32[320]{0:T(512)}, u32[]{:S(2)}) copy-start(f32[320]{0:T(512)} %param.17) | copy-start | bytes 3844
  98.5 21.7 %collective-permute-start.4 = (bf16[1,320,256]{2,1,0:T(8,128)(2,1)S(1)}, bf16[1,320,256]{2,1,0:T(8,128)(2,1)S(1)}, u32[]{:S(2)}, u32[]{:S(2)}) collective-permute-start(bf16[1,320,256]{2,1,0:T(8,128)(2,1)S(1)} %get-tuple-element.10), channel_id=1, source_target_pairs={{0,1},{1,2},{2,3},{3,4},{4,5},{5,6},{6,7},{7,8},{8,9},{9,10},{10,1... | collective-permute-start | bytes 491528 | tf_op jit(solution)/shard_map/ppermute | solution.py:319
  100.4 19.7 %collective-permute-start.5 = (bf16[1,320,256]{2,1,0:T(8,128)(2,1)S(1)}, bf16[1,320,256]{2,1,0:T(8,128)(2,1)S(1)}, u32[]{:S(2)}, u32[]{:S(2)}) collective-permute-start(bf16[1,320,256]{2,1,0:T(8,128)(2,1)S(1)} %get-tuple-element.9), channel_id=1, source_target_pairs={{1,0},{2,1},{3,2},{4,3},{5,4},{6,5},{7,6},{8,7},{9,8},{10,9},{11,1... | collective-permute-start | bytes 491528 | tf_op jit(solution)/shard_map/ppermute | solution.py:320
  104.4 15.8 %all-to-all-start.2 = ((f32[32,1,128]{2,1,0:T(1,128)}), f32[32,1,128]{2,1,0:T(1,128)S(1)}, u32[]{:S(2)}, u32[]{:S(2)}) async-start(f32[32,1,128]{2,1,0:T(1,128)} %get-tuple-element.7), calls=%async_computation.2 | async-start | bytes 32768 | tf_op jit(solution)/shard_map/all_to_all | solution.py:310

commit v2 on v1

v2 whole, which is shorter than its diff:
```python
import jax
import jax.numpy as jnp
from jax import lax
from jax.experimental import pallas as pl
from jax.experimental.pallas import tpu as pltpu
from jax.sharding import Mesh
from jax.sharding import PartitionSpec as P

GROUPS = 32
PER = 10
CU = 320
WIDTH = 256
TAPS = 9
SLABS = TAPS * PER
PAIRS = SLABS // 2
CROWS = 23
CHUNK = 120
ZS, XS = 8, 4
LOCAL = 4.0 * PER * WIDTH
DEPTH = SLABS * GROUPS
ROWK = 1024
ROW = ("row_0", "row_1")
IMG_ROW = ("y", "core", "row_0", "row_1")
EPS = 1e-06

f32 = jnp.float32
bf16 = jnp.bfloat16
ANYWHERE = pl.BlockSpec(memory_space=pl.ANY)
FAR = pl.BlockSpec(memory_space=pltpu.HBM)
WHOLE = pl.BlockSpec(memory_space=pltpu.VMEM)
SCALARS = pl.BlockSpec(memory_space=pltpu.SMEM)
PARAMS = pltpu.CompilerParams(vmem_limit_bytes=24 * 1024 * 1024)


def far(array):
    return pltpu.with_memory_space_constraint(array, pltpu.HBM)


def near(*arrays):
    return [pltpu.with_memory_space_constraint(a, pltpu.VMEM) for a in arrays]


def cost(us):
    return pl.CostEstimate(flops=int(us * 2e8), bytes_accessed=1 << 20, transcendentals=0)


def widen(ref, at, values):
    ref[at : at + CU, :] = values[:, 0:128]
    ref[at + CU : at + 2 * CU, :] = values[:, 128:256]


def slab_of(ref, j, row=0):
    at = row * 2 * CU + j
    halves = [ref[pl.ds(at + n * CU, GROUPS, stride=PER), :] for n in range(2)]
    return jnp.concatenate(halves, axis=1)


def same_slab(ref, j):
    half = ref[pl.ds(j, GROUPS, stride=PER), :]
    return jnp.concatenate([half, half], axis=1)


def local_moments(values, rows):
    total = jnp.zeros((GROUPS, WIDTH), f32)
    for h in range(rows):
        for j in range(PER):
            total += slab_of(values, j, h)
    mean = jnp.sum(total, axis=1, keepdims=True) * (1.0 / (rows * PER * WIDTH))
    off = jnp.zeros((GROUPS, WIDTH), f32)
    for h in range(rows):
        for j in range(PER):
            d = slab_of(values, j, h) - mean
            off += d * d
    return mean, jnp.sum(off, axis=1, keepdims=True)


def turned(column):
    return jnp.transpose(jnp.broadcast_to(column, (column.shape[0], 128)))


def in_three(v):
    hi = v.astype(bf16).astype(f32)
    rest = v - hi
    mid = rest.astype(bf16).astype(f32)
    return hi, mid, rest - mid


def prep_kernel(
    flags_ref, x_hbm, w_hbm, w2_hbm, ch_ref, x_ref, w_ref, w2_ref, wide, flat, chunk, x_sem, w_sem, w2_sem
):
    core = flags_ref[0]
    get_x = pltpu.make_async_copy(x_hbm, x_ref, x_sem)
    get_w = pltpu.make_async_copy(w_hbm, w_ref, w_sem)
    get_w2 = pltpu.make_async_copy(w2_hbm, w2_ref, w2_sem)
    get_w.start()
    get_w2.start()
    get_x.start()
    get_w2.wait()
    fill_chunk(core, w2_ref, flat, chunk)
    whole = chunk[...].astype(bf16)
    for d in range(ZS):
        ch_ref[d, CHUNK : 2 * CHUNK] = whole
    get_w.wait()
    fill_chunk(core, w_ref, flat, chunk)
    get_x.wait()
    for h in range(4):
        widen(wide, h * 2 * CU, x_ref[h].astype(f32))
    mean, off = local_moments(wide, 4)
    rows = [turned(col)[0:1, :] for col in (mean, off)]
    put_stats(rows, chunk)
    whole = chunk[...].astype(bf16)
    for d in range(ZS):
        ch_ref[d, 0:CHUNK] = whole


def put_stats(rows, chunk):
    for k, row in enumerate(rows):
        for n, piece in enumerate(in_three(row[:, 0:GROUPS])):
            at = SLABS + CROWS + 3 * k + n
            chunk[at : at + 1, 0:GROUPS] = piece


def got_stats(tail):
    piece = lambda n: tail[:, n, 0:GROUPS]
    return piece(1) + piece(2) + piece(3), piece(4) + piece(5) + piece(6)


def pooled(means, offs, count):
    n = means.shape[0]
    mean = jnp.sum(means, axis=0, keepdims=True) * (1.0 / n)
    d = means - mean
    return mean, jnp.sum(offs, axis=0, keepdims=True) + count * jnp.sum(d * d, axis=0, keepdims=True)


def middle_kernel(g_ref, above_ref, below_ref, xch_ref, w2_ref, tail):
    rows = pooled(*got_stats(g_ref[:, CHUNK - 8 : CHUNK, :].astype(f32)), LOCAL)
    tail[...] = g_ref[0, 0:CHUNK, :].astype(f32)
    put_stats(rows, tail)
    first = tail[...].astype(bf16)
    for d in range(XS):
        xch_ref[d, 0] = first
        for z in range(1, ZS):
            xch_ref[d, z] = g_ref[z, 0:CHUNK, :]
    for z in range(ZS):
        w2_ref[z] = g_ref[z, CHUNK : 2 * CHUNK, :]


def middle(got, above, below):
    return pl.pallas_call(
        middle_kernel,
        out_shape=(
            jax.ShapeDtypeStruct((XS, ZS, CHUNK, 128), bf16),
            pltpu.VMEM((ZS, CHUNK, 128), bf16),
        ),
        in_specs=[WHOLE, ANYWHERE, ANYWHERE],
        out_specs=(WHOLE, WHOLE),
        scratch_shapes=[pltpu.VMEM((CHUNK, 128), f32)],
        compiler_params=PARAMS,
        cost_estimate=cost(1),
        name="middle",
    )(got, above, below)


def join_kernel(flags_ref, own_ref, a_ref, b_ref, c_ref, after_ref, out_ref):
    x = flags_ref[3]
    for s, ref in enumerate((own_ref, a_ref, b_ref, c_ref)):
        at = (x + XS - s) % XS
        for z in range(ZS):
            out_ref[z * XS + at] = ref[z]


def join(flags, pieces, after):
    return pl.pallas_call(
        join_kernel,
        out_shape=pltpu.VMEM((GROUPS, CHUNK, 128), bf16),
        in_specs=[SCALARS] + [WHOLE] * 4 + [ANYWHERE],
        out_specs=WHOLE,
        compiler_params=PARAMS,
        cost_estimate=cost(1),
        name="join",
    )(flags, *near(*pieces), after)


def fill_chunk(core, w_ref, flat, chunk):
    for p in range(3):
        for j in range(PER):
            at = (p * PER + j) * 3
            flat[at : at + 3, 0:CU] = w_ref[p, j].astype(f32)
    chunk[...] = jnp.zeros((CHUNK, 128), f32)
    first = core == 0
    chunk[0:SLABS, :] = jnp.where(first, flat[0:SLABS, 0:128], flat[0:SLABS, 128:256])
    for c in range(2):
        t0 = (CROWS - 1) * c
        lo = flat[t0 : t0 + CROWS, 256:384]
        hi = pltpu.roll(flat[PAIRS + t0 : PAIRS + t0 + CROWS, 256:384], 64, 1)
        lane = lax.broadcasted_iota(jnp.int32, (CROWS, 128), 1)
        both = jnp.where(lane < 64, lo, hi)

        @pl.when(core == c)
        def _():
            chunk[SLABS : SLABS + CROWS, :] = both


def prep(flags, *arrays):
    arrays = [far(a) for a in arrays]
    return pl.pallas_call(
        prep_kernel,
        out_shape=jax.ShapeDtypeStruct((ZS, 2 * CHUNK, 128), bf16),
        in_specs=[SCALARS] + [FAR] * 3,
        out_specs=WHOLE,
        scratch_shapes=[
            pltpu.VMEM((4, CU, WIDTH), bf16),
            pltpu.VMEM((3, PER, 3, CU), bf16),
            pltpu.VMEM((3, PER, 3, CU), bf16),
            pltpu.VMEM((8 * CU, 128), f32),
            pltpu.VMEM((96, 384), f32),
            pltpu.VMEM((CHUNK, 128), f32),
            pltpu.SemaphoreType.DMA,
            pltpu.SemaphoreType.DMA,
            pltpu.SemaphoreType.DMA,
        ],
        compiler_params=PARAMS,
        cost_estimate=cost(3),
        name="prep",
    )(flags, *arrays)


def column_of(row):
    return jnp.transpose(jnp.broadcast_to(row, (128, row.shape[1])))


def combine(means, offs, count):
    center, off = pooled(means, offs, count)
    inv = lax.rsqrt(off * (1.0 / (means.shape[0] * count)) + EPS)
    return column_of(center), column_of(inv)


def activate(flags_ref, rows, center, inv, gain_ref, beta_ref, cols, wide, act_ref):
    gains, betas = cols
    gains[...] = column_of(gain_ref[...])
    betas[...] = column_of(beta_ref[...])
    two = lambda a: jnp.concatenate([a, a], axis=1)
    center, inv = two(center), two(inv)
    lane = lax.broadcasted_iota(jnp.int32, (GROUPS, WIDTH), 1)
    for h in (1, 2, 3, 4, 0, 5):
        act_ref[h * ROWK + 3 * CU : (h + 1) * ROWK, :] = jnp.zeros((ROWK - 3 * CU, WIDTH), bf16)
        widen(wide, 0, rows(h).astype(f32))
        for j in range(PER):
            v = (slab_of(wide, j) - center) * inv
            v = v * same_slab(gains, j) + same_slab(betas, j)
            v = v / (1.0 + jnp.exp(-v))
            if h == 0:
                v = jnp.where(flags_ref[1] == 0, 0.0, v)
            if h == 5:
                v = jnp.where(flags_ref[2] == 0, 0.0, v)
            left = jnp.where(lane == 0, 0.0, pltpu.roll(v, 1, 1))
            right = jnp.where(lane == WIDTH - 1, 0.0, pltpu.roll(v, WIDTH - 1, 1))
            at = h * ROWK + j * 3 * GROUPS
            act_ref[at : at + GROUPS, :] = left.astype(bf16)
            act_ref[at + GROUPS : at + 2 * GROUPS, :] = v.astype(bf16)
            act_ref[at + 2 * GROUPS : at + 3 * GROUPS, :] = right.astype(bf16)


def fetched(fars, here, sems):
    copies = [pltpu.make_async_copy(far_ref, here.at[n], sems.at[n]) for n, far_ref in enumerate(fars)]
    for copy in copies:
        copy.start()

    def get(n):
        copies[n].wait()
        return here[n]

    return get


def norm1_kernel(
    flags_ref, g_ref, top_hbm, mid_ref, bot_hbm, gain_ref, beta_ref, act_ref, wt_ref, gains, betas, wide, many, here, sems
):
    edge = fetched((top_hbm.at[0], bot_hbm.at[0]), here, sems)
    own_block(g_ref, many, wt_ref)
    center, inv = combine(*got_stats(g_ref[:, 0, CHUNK - 8 : CHUNK, :].astype(f32)), ZS * LOCAL)
    rows = lambda h: mid_ref[h - 1] if 0 < h < 5 else edge(int(h == 5))
    activate(flags_ref, rows, center, inv, gain_ref, beta_ref, (gains, betas), wide, act_ref)


def norm2_kernel(
    flags_ref, s_ref, top_ref, mid_hbm, bot_ref, gain_ref, beta_ref, act_ref, gains, betas, wide, here, sems
):
    middle_row = fetched([mid_hbm.at[h] for h in range(4)], here, sems)
    both = s_ref[:, 0, :]
    center, inv = combine(both[:, 0:GROUPS], both[:, GROUPS : 2 * GROUPS], LOCAL)
    rows = lambda h: middle_row(h - 1) if 0 < h < 5 else (bot_ref if h else top_ref)[0]
    activate(flags_ref, rows, center, inv, gain_ref, beta_ref, (gains, betas), wide, act_ref)


NORM_SCRATCH = [
    pltpu.VMEM((CU, 128), f32),
    pltpu.VMEM((CU, 128), f32),
    pltpu.VMEM((2 * CU, 128), f32),
]
MANY = pltpu.VMEM((GROUPS * CHUNK, 128), f32)
ACT = pltpu.VMEM((6 * ROWK, WIDTH), bf16)


def rows_here(n):
    return [pltpu.VMEM((n, CU, WIDTH), bf16), pltpu.SemaphoreType.DMA((n,))]


def norm1(flags, own, top, mid, bot, gain, beta):
    return pl.pallas_call(
        norm1_kernel,
        out_shape=(ACT, pltpu.VMEM((128, 3 * ROWK), bf16)),
        in_specs=[SCALARS, WHOLE, FAR, WHOLE, FAR, WHOLE, WHOLE],
        out_specs=(WHOLE, WHOLE),
        scratch_shapes=NORM_SCRATCH + [MANY] + rows_here(2),
        compiler_params=PARAMS,
        cost_estimate=cost(3),
        name="norm1",
    )(flags, *near(own), far(top), mid, far(bot), gain.reshape(1, CU), beta.reshape(1, CU))


def norm2(flags, stats, top, mid, bot, gain, beta):
    return pl.pallas_call(
        norm2_kernel,
        out_shape=ACT,
        in_specs=[SCALARS, WHOLE, WHOLE, FAR, WHOLE, WHOLE, WHOLE],
        out_specs=WHOLE,
        scratch_shapes=NORM_SCRATCH + rows_here(4),
        compiler_params=PARAMS,
        cost_estimate=cost(2),
        name="norm2",
    )(flags, stats, top, far(mid), bot, gain.reshape(1, CU), beta.reshape(1, CU))


def shard_at(g_ref, d, rows):
    part = g_ref[d, rows, :] if len(g_ref.shape) == 3 else g_ref[d % XS, d // XS, rows, :]
    return part.astype(f32)


def spread_out(g_ref, many):
    for d in range(GROUPS):
        many[d * CHUNK : (d + 1) * CHUNK, :] = shard_at(g_ref, d, slice(0, CHUNK))


def block(many):
    out = []
    for p in range(3):
        slabs = [many[pl.ds(p * 30 + m, GROUPS, stride=CHUNK), :].astype(bf16) for m in range(30)]
        slabs.append(jnp.zeros((ROWK - 3 * CU, 128), bf16))
        out.append(jnp.transpose(jnp.concatenate(slabs, axis=0)))
    return out


def own_block(g_ref, many, wt_ref):
    spread_out(g_ref, many)
    for p, part in enumerate(block(many)):
        wt_ref[:, p * ROWK : (p + 1) * ROWK] = part


def rest_of(core, many, w):
    t0 = core * (CROWS - 1)
    for t in range(CROWS):
        v = many[pl.ds(SLABS + t, GROUPS, stride=CHUNK), :]
        at = pl.multiple_of((t0 + t) * GROUPS, GROUPS)
        w[pl.ds(at, GROUPS), :] = v.astype(bf16)
        w[pl.ds(at + PAIRS * GROUPS, GROUPS), :] = pltpu.roll(v, 64, 1).astype(bf16)


def rest_turned(w, wt):
    for p in range(3):
        part = jnp.concatenate([w[p * 3 * CU : (p + 1) * 3 * CU, :], jnp.zeros((ROWK - 3 * CU, 128), bf16)], axis=0)
        wt[256:CU, p * ROWK : (p + 1) * ROWK] = jnp.transpose(part)[0:64, :]


def rows_of(core):
    return pl.ds(pl.multiple_of(core * 128, 128), 128)


def conv_row(h, act_ref, wt):
    return jnp.dot(wt[...], act_ref[h * ROWK : (h + 3) * ROWK, :], preferred_element_type=f32)


def all_weights(flags_ref, own_ref, wto_ref, other_ref, many, many2, w, wt):
    core = flags_ref[0]
    for d in range(GROUPS):
        many2[d * 32 : (d + 1) * 32, :] = shard_at(own_ref, d, slice(CHUNK - 32, CHUNK))
    t0 = core * (CROWS - 1)
    for t in range(CROWS):
        v = many2[pl.ds(2 + t, GROUPS, stride=32), :]
        at = pl.multiple_of((t0 + t) * GROUPS, GROUPS)
        w[pl.ds(at, GROUPS), :] = v.astype(bf16)
        w[pl.ds(at + PAIRS * GROUPS, GROUPS), :] = pltpu.roll(v, 64, 1).astype(bf16)
    spread_out(other_ref, many)
    rest_of(1 - core, many, w)
    rest_turned(w, wt)
    wt[rows_of(core), :] = wto_ref[...]
    for p, part in enumerate(block(many)):
        wt[rows_of(1 - core), p * ROWK : (p + 1) * ROWK] = part


def conv1_kernel(
    flags_ref, own_ref, wto_ref, other_ref, act_ref, shift_ref, hid_hbm, first_hbm, last_hbm, st_ref, many, many2, w, wt, full, hid, sems
):
    all_weights(flags_ref, own_ref, wto_ref, other_ref, many, many2, w, wt)
    shift = column_of(shift_ref[...])
    shift = jnp.concatenate([shift, shift], axis=1)
    for h in range(4):
        row = (conv_row(h, act_ref, wt) + shift).astype(bf16)
        hid[h] = row
        widen(full, h * 2 * CU, row.astype(f32))
    puts = [
        pltpu.make_async_copy(hid.at[0:1], first_hbm, sems.at[0]),
        pltpu.make_async_copy(hid.at[3:4], last_hbm, sems.at[1]),
        pltpu.make_async_copy(hid, hid_hbm, sems.at[2]),
    ]
    for put in puts:
        put.start()
    mean, off = local_moments(full, 4)
    line = turned(jnp.concatenate([mean, off], axis=0))[0:1, :]
    line = jnp.concatenate([line, jnp.zeros((1, 64), f32)], axis=1)
    for d in range(GROUPS):
        st_ref[d] = line
    for put in puts:
        put.wait()


WT = (CU, 3 * ROWK)
CONV_SCRATCH = [
    MANY,
    pltpu.VMEM((GROUPS * 32, 128), f32),
    pltpu.VMEM((DEPTH, 128), bf16),
    pltpu.VMEM(WT, bf16),
]


def conv1(flags, own, wto, other, act, shift):
    edge = pltpu.HBM((1, CU, WIDTH), bf16)
    return pl.pallas_call(
        conv1_kernel,
        out_shape=(
            pltpu.HBM((4, CU, WIDTH), bf16),
            edge,
            edge,
            jax.ShapeDtypeStruct((GROUPS, 1, 128), f32),
        ),
        in_specs=[SCALARS] + [WHOLE] * 5,
        out_specs=(FAR, FAR, FAR, WHOLE),
        scratch_shapes=CONV_SCRATCH
        + [
            pltpu.VMEM((8 * CU, 128), f32),
            pltpu.VMEM((4, CU, WIDTH), bf16),
            pltpu.SemaphoreType.DMA((3,)),
        ],
        compiler_params=PARAMS,
        cost_estimate=cost(5),
        name="conv1",
    )(flags, *near(own, wto, other, act), shift.reshape(1, CU))


def own2_kernel(own_ref, wt_ref, many):
    own_block(own_ref, many, wt_ref)


def own2_part(own):
    return pl.pallas_call(
        own2_kernel,
        out_shape=pltpu.VMEM((128, 3 * ROWK), bf16),
        in_specs=[WHOLE],
        out_specs=WHOLE,
        scratch_shapes=[MANY],
        compiler_params=PARAMS,
        cost_estimate=cost(1),
        name="own2",
    )(*near(own))


def conv2_kernel(flags_ref, own_ref, wto_ref, other_ref, act_ref, bias_ref, x_ref, out_ref, many, many2, w, wt):
    all_weights(flags_ref, own_ref, wto_ref, other_ref, many, many2, w, wt)
    bias = column_of(bias_ref[...])
    bias = jnp.concatenate([bias, bias], axis=1)
    for h in range(4):
        out_ref[h] = (x_ref[h].astype(f32) + (conv_row(h, act_ref, wt) + bias)).astype(bf16)


def conv2(flags, own, wto, other, act, bias, x):
    return pl.pallas_call(
        conv2_kernel,
        out_shape=jax.ShapeDtypeStruct((4, CU, WIDTH), bf16),
        in_specs=[SCALARS] + [WHOLE] * 6,
        out_specs=WHOLE,
        scratch_shapes=CONV_SCRATCH,
        compiler_params=PARAMS,
        cost_estimate=cost(4),
        name="conv2",
    )(flags, *near(own, wto, other, act), bias.reshape(1, CU), *near(x))


def to_all(chunks, axis):
    return lax.all_to_all(chunks, axis, 0, 0, tiled=True)


def swapped(chunks):
    return lax.ppermute(chunks, "core", [(0, 1), (1, 0)])


def edges(first, last):
    count = lax.axis_size(ROW)
    above = lax.ppermute(last, ROW, [(i, i + 1) for i in range(count - 1)])
    below = lax.ppermute(first, ROW, [(i + 1, i) for i in range(count - 1)])
    return above, below


def block_of(
    lat_pixels,
    first_gain,
    first_beta,
    first_kernel,
    time_shift,
    second_gain,
    second_beta,
    second_kernel,
    second_bias,
):
    x = lat_pixels.transpose(0, 2, 1)
    place = lax.axis_index(ROW)
    last = lax.axis_size(ROW) - 1
    flags = jnp.stack(
        [lax.axis_index("core"), (place > 0).astype(jnp.int32), (place < last).astype(jnp.int32), place % XS]
    ).astype(jnp.int32)
    chunks = prep(flags, x, first_kernel.transpose(0, 2, 1, 3), second_kernel.transpose(0, 2, 1, 3))
    got = to_all(chunks, "row_0")
    above, below = edges(x[0:1], x[3:4])
    xch, w2z = middle(got, above, below)
    own1 = to_all(xch, "row_1")
    pieces = [w2z]
    for s in range(1, XS):
        pieces.append(lax.ppermute(w2z, "row_1", [(i, (i + s) % XS) for i in range(XS)]))
    other1 = swapped(own1)
    act, wto = norm1(flags, own1, above, x, below, first_gain, first_beta)
    hidden, first, last, st = conv1(flags, own1, wto, other1, act, time_shift)
    stats = to_all(st, ROW)
    habove, hbelow = edges(first, last)
    own2 = join(flags, pieces, st)
    other2 = swapped(own2)
    wto2 = own2_part(own2)
    act2 = norm2(flags, stats, habove, hidden, hbelow, second_gain, second_beta)
    out = conv2(flags, own2, wto2, other2, act2, second_bias, x)
    return out.transpose(0, 2, 1)


def solution(mesh):
    split = Mesh(mesh.devices.reshape(mesh.shape["img"] // 2, 2, 8, 4), ("y", "core", "row_0", "row_1"))
    placed = (
        P(IMG_ROW, None, None),
        P(),
        P(),
        P(None, None, ROW, None),
        P(("y", "core")),
        P(),
        P(),
        P(None, None, ROW, None),
        P(),
    )
    return jax.shard_map(block_of, mesh=split, in_specs=placed, out_specs=P(IMG_ROW, None, None), check_vma=False)
```

time: 130 us -> 106 us (0.82)
  waiting for transfers between devices: 63.9 us -> 21.8 us
  blocking collectives: 0 us -> 17.2 us
  local copies, waits for them, and re-layouts: 3.04 us -> 0.08 us
  Pallas kernels: 17.9 us -> 20.1 us
  starting transfers between devices: 42.5 us -> 44.7 us
    all_to_all x3 -> x2, waiting for transfers between devices: 56.5 us -> 7.91 us  [to_all(): return lax.all_to_all(chunks, axis, 0, 0, tiled=True)]
    all_to_all x0 -> x1, blocking collectives: none -> 17.2 us  [to_all(): return lax.all_to_all(chunks, axis, 0, 0, tiled=True)]
    ppermute x4 -> x7, starting transfers between devices: 11.7 us -> 20.9 us  [the longest x3 9.21 us: block_of(): lax.ppermute(w2z, 'row_1', [(i, (i + s) % XS) for i in range(XS)])]
    all_to_all x3 -> x2, starting transfers between devices: 27 us -> 20 us  [to_all(): return lax.all_to_all(chunks, axis, 0, 0, tiled=True)]
    ppermute x4 -> x7, waiting for transfers between devices: 7.38 us -> 13.9 us  [the longest x2 8.34 us: edges(): above = lax.ppermute(last, ROW, [(i, i + 1) for i in range(count - 1)])]
    unnamed x22 -> x18, local copies, waits for them, and re-layouts: 2.98 us -> 0.04 us
    pallas_call x5 -> x7, Pallas kernels: 12.6 us -> 15.5 us  [the longest x1 5.44 us: conv1(): pl.pallas_call(conv1_kernel, out_shape=(pltpu.HBM((4, CU, WIDTH), bf16),...]
  transfers between devices with their start and end apart: 9 -> 11, of which waited for: 5 -> 5; matrix products, arithmetic and copies ran while one was open for 0% -> 0% of each run, Pallas kernels for 8% -> 11%
where the time goes in v2:
time: 106 us; the launch traced here: 104 us
  starting transfers between devices  44.7 us (42%)
  waiting for transfers between devices  21.8 us (21%)
  Pallas kernels  20.1 us (19%)
  blocking collectives  17.2 us (16%)
    all_to_all x2, starting transfers between devices, to_all(): return lax.all_to_all(chunks, axis, 0, 0, tiled=True)  20 us
    all_to_all x1, blocking collectives, to_all(): return lax.all_to_all(chunks, axis, 0, 0, tiled=True)  17.2 us
    ppermute x3, starting transfers between devices, block_of(): lax.ppermute(w2z, 'row_1', [(i, (i + s) % XS) for i in range(XS)])  9.21 us
    ppermute x2, waiting for transfers between devices, edges(): above = lax.ppermute(last, ROW, [(i, i + 1) for i in range(count - 1)])  8.34 us
    all_to_all x2, waiting for transfers between devices, to_all(): return lax.all_to_all(chunks, axis, 0, 0, tiled=True)  7.91 us
    ppermute x2, starting transfers between devices, edges(): below = lax.ppermute(first, ROW, [(i + 1, i) for i in range(count - 1)])  5.93 us
    ppermute x2, starting transfers between devices, edges(): above = lax.ppermute(last, ROW, [(i, i + 1) for i in range(count - 1)])  5.76 us
    pallas_call x1, Pallas kernels, conv1(): pl.pallas_call(conv1_kernel, out_shape=(pltpu.HBM((4, CU, WIDTH), bf16),...  5.44 us
  transfers between devices with their start and end apart: 11, of which 5 were waited for; matrix products, arithmetic and copies ran while one was open for 0% of the time, Pallas kernels for 11%

profile of v2, /device:TPU:6, one launch (start us, length us, event | category | flops | bytes accessed | tf_op | source)
XLA Modules:
  0.0 104.3 jit_solution(9561428884786820022)
XLA Ops:
  0.1 3.1 %prep.1 = bf16[8,240,128]{2,1,0:T(8,128)(2,1)} custom-call(s32[4]{0:T(128)S(1)} %pad_add_fusion.flags_ref, bf16[4,320,256]{2,1,0:T(8,128)(2,1)} %bitcast.8, bf16[3,10,3,320]{3,2,1,0:T(4,128)(2,1)} %bitcast.12, bf16[3,10,3,320]{3,2,1,0:T(4,128)(2,1)} %bitcast.13), custom_call_target="tpu_custom_call" | custom-call | flops 600000000 | bytes 1048576 | tf_op jit(solution)/shard_map/prep/pallas_call | solution.py:206
  3.2 10.3 %all-to-all-start = ((bf16[8,240,128]{2,1,0:T(8,128)(2,1)}), bf16[8,240,128]{2,1,0:T(8,128)(2,1)S(1)}, u32[]{:S(2)}, u32[]{:S(2)}) async-start(bf16[8,240,128]{2,1,0:T(8,128)(2,1)} %prep.1), calls=%async_computation | async-start | bytes 983040 | tf_op jit(solution)/shard_map/all_to_all | solution.py:499
  13.5 3.8 %collective-permute-start = (bf16[1,320,256]{2,1,0:T(8,128)(2,1)S(1)}, bf16[1,320,256]{2,1,0:T(8,128)(2,1)S(1)}, u32[]{:S(2)}, u32[]{:S(2)}) collective-permute-start(bf16[1,320,256]{2,1,0:T(8,128)(2,1)S(1)} %get-tuple-element.22), channel_id=1, source_target_pairs={{0,1},{1,2},{2,3},{3,4},{4,5},{5,6},{6,7},{7,8},{8,9},{9,10},{10,1... | collective-permute-start | bytes 491528 | tf_op jit(solution)/shard_map/ppermute | solution.py:508
  17.4 2.0 %collective-permute-start.1 = (bf16[1,320,256]{2,1,0:T(8,128)(2,1)S(1)}, bf16[1,320,256]{2,1,0:T(8,128)(2,1)S(1)}, u32[]{:S(2)}, u32[]{:S(2)}) collective-permute-start(bf16[1,320,256]{2,1,0:T(8,128)(2,1)S(1)} %get-tuple-element.21), channel_id=1, source_target_pairs={{1,0},{2,1},{3,2},{4,3},{5,4},{6,5},{7,6},{8,7},{9,8},{10,9},{11,1... | collective-permute-start | bytes 491528 | tf_op jit(solution)/shard_map/ppermute | solution.py:509
  19.4 8.3 %collective-permute-done.above_ref.top_hbm = bf16[1,320,256]{2,1,0:T(8,128)(2,1)S(1)} collective-permute-done((bf16[1,320,256]{2,1,0:T(8,128)(2,1)S(1)}, bf16[1,320,256]{2,1,0:T(8,128)(2,1)S(1)}, u32[]{:S(2)}, u32[]{:S(2)}) %collective-permute-start) | collective-permute-done | bytes 163872 | tf_op jit(solution)/shard_map/ppermute | solution.py:508
  27.7 2.1 %collective-permute-done.1.below_ref.bot_hbm = bf16[1,320,256]{2,1,0:T(8,128)(2,1)S(1)} collective-permute-done((bf16[1,320,256]{2,1,0:T(8,128)(2,1)S(1)}, bf16[1,320,256]{2,1,0:T(8,128)(2,1)S(1)}, u32[]{:S(2)}, u32[]{:S(2)}) %collective-permute-start.1) | collective-permute-done | bytes 163872 | tf_op jit(solution)/shard_map/ppermute | solution.py:509
  29.8 0.3 all-to-all-done.g_ref
  30.3 17.2 %all_to_all.15.g_ref.own_ref = bf16[4,8,120,128]{3,2,1,0:T(8,128)(2,1)S(1)} all-to-all(bf16[4,8,120,128]{3,2,1,0:T(8,128)(2,1)S(1)} %get-tuple-element.14), channel_id=1, replica_groups=mesh['y'=8,'core'=2,'row_0'=8,'row_1'=4] {'row_1'}, dimensions={0} | all-to-all | bytes 1966080 | tf_op jit(solution)/shard_map/all_to_all | solution.py:499
  47.5 1.9 %collective-permute-start.5 = (bf16[4,8,120,128]{3,2,1,0:T(8,128)(2,1)S(1)}, bf16[4,8,120,128]{3,2,1,0:T(8,128)(2,1)S(1)}, u32[]{:S(2)}, u32[]{:S(2)}) collective-permute-start(bf16[4,8,120,128]{3,2,1,0:T(8,128)(2,1)S(1)} %all_to_all.15.g_ref.own_ref), channel_id=1, source_target_pairs={{0,32},{32,0},{1,33},{33,1},{2,34},{34,2},{3,35},{35,3},{4,36},{36... | collective-permute-start | bytes 2949128 | tf_op jit(solution)/shard_map/ppermute | solution.py:503
  49.4 4.0 %collective-permute-start.2 = (bf16[8,120,128]{2,1,0:T(8,128)(2,1)S(1)}, bf16[8,120,128]{2,1,0:T(8,128)(2,1)S(1)}, u32[]{:S(2)}, u32[]{:S(2)}) collective-permute-start(bf16[8,120,128]{2,1,0:T(8,128)(2,1)S(1)} %get-tuple-element.13.own_ref), channel_id=1, source_target_pairs={{0,1},{1,2},{2,3},{3,0},{4,5},{5,6},{6,7},{7,4},{8,9},{9,10},{10,1... | collective-permute-start | bytes 737288 | tf_op jit(solution)/shard_map/ppermute | solution.py:537
  53.4 2.3 %collective-permute-start.3 = (bf16[8,120,128]{2,1,0:T(8,128)(2,1)S(1)}, bf16[8,120,128]{2,1,0:T(8,128)(2,1)S(1)}, u32[]{:S(2)}, u32[]{:S(2)}) collective-permute-start(bf16[8,120,128]{2,1,0:T(8,128)(2,1)S(1)} %get-tuple-element.13.own_ref), channel_id=1, source_target_pairs={{0,2},{1,3},{2,0},{3,1},{4,6},{5,7},{6,4},{7,5},{8,10},{9,11},{10,... | collective-permute-start | bytes 737288 | tf_op jit(solution)/shard_map/ppermute | solution.py:537
  55.7 2.9 %collective-permute-start.4 = (bf16[8,120,128]{2,1,0:T(8,128)(2,1)S(1)}, bf16[8,120,128]{2,1,0:T(8,128)(2,1)S(1)}, u32[]{:S(2)}, u32[]{:S(2)}) collective-permute-start(bf16[8,120,128]{2,1,0:T(8,128)(2,1)S(1)} %get-tuple-element.13.own_ref), channel_id=1, source_target_pairs={{0,3},{1,0},{2,1},{3,2},{4,7},{5,4},{6,5},{7,6},{8,11},{9,8},{10,9... | collective-permute-start | bytes 737288 | tf_op jit(solution)/shard_map/ppermute | solution.py:537
  58.8 2.4 %norm1.1 = (bf16[6144,256]{1,0:T(8,128)(2,1)S(1)}, bf16[128,3072]{1,0:T(8,128)(2,1)S(1)}) custom-call(s32[4]{0:T(128)S(1)} %pad_add_fusion.flags_ref, bf16[4,8,120,128]{3,2,1,0:T(8,128)(2,1)S(1)} %all_to_all.15.g_ref.own_ref, bf16[1,320,256]{2,1,0:T(8,128)(2,1)} %copy-done.1, bf16[4,320,256]{2,1,0:T(8,128)(2,1)S(1)} %bitcast.10, ...), custom_call_target="tpu_custom_call" | custom-call | flops 600000000 | bytes 1048576 | tf_op jit(solution)/shard_map/norm1/pallas_call | solution.py:310
  61.2 5.4 %conv1.1 = (bf16[4,320,256]{2,1,0:T(8,128)(2,1)}, bf16[1,320,256]{2,1,0:T(8,128)(2,1)}, bf16[1,320,256]{2,1,0:T(8,128)(2,1)}, f32[32,1,128]{2,1,0:T(1,128)}) custom-call(s32[4]{0:T(128)S(1)} %pad_add_fusion.flags_ref, bf16[4,8,120,128]{3,2,1,0:T(8,128)(2,1)S(1)} %all_to_all.15.g_ref.own_ref, bf16[128,3072]{1,0:T(8,128)(2,1)S(1)} %get-tuple-element.15.wto_ref, ...), custom_call_target="tpu_custom_call" | custom-call | flops 1000000000 | bytes 1048576 | tf_op jit(solution)/shard_map/conv1/pallas_call | solution.py:438
  66.7 3.5 %collective-permute-done.4.c_ref = bf16[8,120,128]{2,1,0:T(8,128)(2,1)S(1)} collective-permute-done((bf16[8,120,128]{2,1,0:T(8,128)(2,1)S(1)}, bf16[8,120,128]{2,1,0:T(8,128)(2,1)S(1)}, u32[]{:S(2)}, u32[]{:S(2)}) %collective-permute-start.4) | collective-permute-done | bytes 245792 | tf_op jit(solution)/shard_map/ppermute | solution.py:537
  70.2 0.6 join.1.own_ref
  70.8 1.9 %collective-permute-start.6 = (bf16[32,120,128]{2,1,0:T(8,128)(2,1)S(1)}, bf16[32,120,128]{2,1,0:T(8,128)(2,1)S(1)}, u32[]{:S(2)}, u32[]{:S(2)}) collective-permute-start(bf16[32,120,128]{2,1,0:T(8,128)(2,1)S(1)} %join.1.own_ref), channel_id=1, source_target_pairs={{0,32},{32,0},{1,33},{33,1},{2,34},{34,2},{3,35},{35,3},{4,36},{36... | collective-permute-start | bytes 2949128 | tf_op jit(solution)/shard_map/ppermute | solution.py:503
  72.7 1.9 %collective-permute-start.7 = (bf16[1,320,256]{2,1,0:T(8,128)(2,1)}, bf16[1,320,256]{2,1,0:T(8,128)(2,1)}, u32[]{:S(2)}, u32[]{:S(2)}) collective-permute-start(bf16[1,320,256]{2,1,0:T(8,128)(2,1)} %get-tuple-element.18), channel_id=1, source_target_pairs={{0,1},{1,2},{2,3},{3,4},{4,5},{5,6},{6,7},{7,8},{8,9},{9,10},{10,1... | collective-permute-start | bytes 491528 | tf_op jit(solution)/shard_map/ppermute | solution.py:508
  74.6 3.9 %collective-permute-start.8 = (bf16[1,320,256]{2,1,0:T(8,128)(2,1)}, bf16[1,320,256]{2,1,0:T(8,128)(2,1)}, u32[]{:S(2)}, u32[]{:S(2)}) collective-permute-start(bf16[1,320,256]{2,1,0:T(8,128)(2,1)} %get-tuple-element.20), channel_id=1, source_target_pairs={{1,0},{2,1},{3,2},{4,3},{5,4},{6,5},{7,6},{8,7},{9,8},{10,9},{11,1... | collective-permute-start | bytes 491528 | tf_op jit(solution)/shard_map/ppermute | solution.py:509
  78.6 9.7 %all-to-all-start.2 = ((f32[32,1,128]{2,1,0:T(1,128)}), f32[32,1,128]{2,1,0:T(1,128)S(1)}, u32[]{:S(2)}, u32[]{:S(2)}) async-start(f32[32,1,128]{2,1,0:T(1,128)} %get-tuple-element.17.after_ref), calls=%async_computation.2 | async-start | bytes 32768 | tf_op jit(solution)/shard_map/all_to_all | solution.py:499
  88.3 0.4 own2.1.wto_ref
  88.7 7.6 %all-to-all-done.2.s_ref = f32[32,1,128]{2,1,0:T(1,128)S(1)} async-done(((f32[32,1,128]{2,1,0:T(1,128)}), f32[32,1,128]{2,1,0:T(1,128)S(1)}, u32[]{:S(2)}, u32[]{:S(2)}) %all-to-all-start.2) | async-done | bytes 16416 | tf_op jit(solution)/shard_map/all_to_all | solution.py:499
  96.3 3.4 %norm2.1.act_ref = bf16[6144,256]{1,0:T(8,128)(2,1)S(1)} custom-call(s32[4]{0:T(128)S(1)} %pad_add_fusion.flags_ref, f32[32,1,128]{2,1,0:T(1,128)S(1)} %all-to-all-done.2.s_ref, bf16[1,320,256]{2,1,0:T(8,128)(2,1)} %collective-permute-done.7.top_ref, bf16[4,320,256]{2,1,0:T(8,128)(2,1)} %get-tuple-element.19.mid_hbm, ...), custom_call_target="tpu_custom_call" | custom-call | flops 400000000 | bytes 1048576 | tf_op jit(solution)/shard_map/norm2/pallas_call | solution.py:323
  99.7 4.6 %conv2.1 = bf16[4,320,256]{2,1,0:T(8,128)(2,1)} custom-call(s32[4]{0:T(128)S(1)} %pad_add_fusion.flags_ref, bf16[32,120,128]{2,1,0:T(8,128)(2,1)S(1)} %join.1.own_ref, bf16[128,3072]{1,0:T(8,128)(2,1)S(1)} %own2.1.wto_ref, bf16[32,120,128]{2,1,0:T(8,128)(2,1)S(1)} %collective-permute-done.6.other_ref, bf16[6144,256]{1,0:T(8,128)(2,1)S(1)} %norm2.1.act_ref, ...), custom_call_target="tpu_custom_call" | custom-call | flops 800000000 | bytes 1048576 | tf_op jit(solution)/shard_map/conv2/pallas_call | solution.py:486
  (33 shorter events, 0.3 us)
Async XLA Ops:
  0.0 13.5 %copy-start = (bf16[4,256,320]{1,2,0:T(8,128)(2,1)S(1)}, bf16[4,256,320]{1,2,0:T(8,128)(2,1)}, u32[]{:S(2)}) copy-start(bf16[4,256,320]{1,2,0:T(8,128)(2,1)} %param.9) | copy-start | bytes 1966084
  0.1 58.6 %copy-start.3 = (f32[320]{0:T(512)S(1)}, f32[320]{0:T(512)}, u32[]{:S(2)}) copy-start(f32[320]{0:T(512)} %param.10) | copy-start | bytes 3844
  0.1 58.6 %copy-start.4 = (f32[320]{0:T(512)S(1)}, f32[320]{0:T(512)}, u32[]{:S(2)}) copy-start(f32[320]{0:T(512)} %param.11) | copy-start | bytes 3844
  0.1 58.6 %copy-start.5 = (f32[320]{0:T(512)S(1)}, f32[320]{0:T(512)}, u32[]{:S(2)}) copy-start(f32[320]{0:T(512)} %param.13) | copy-start | bytes 3844
  3.2 27.0 %all-to-all-start = ((bf16[8,240,128]{2,1,0:T(8,128)(2,1)}), bf16[8,240,128]{2,1,0:T(8,128)(2,1)S(1)}, u32[]{:S(2)}, u32[]{:S(2)}) async-start(bf16[8,240,128]{2,1,0:T(8,128)(2,1)} %prep.1), calls=%async_computation | async-start | bytes 983040 | tf_op jit(solution)/shard_map/all_to_all | solution.py:499
  13.5 14.2 %collective-permute-start = (bf16[1,320,256]{2,1,0:T(8,128)(2,1)S(1)}, bf16[1,320,256]{2,1,0:T(8,128)(2,1)S(1)}, u32[]{:S(2)}, u32[]{:S(2)}) collective-permute-start(bf16[1,320,256]{2,1,0:T(8,128)(2,1)S(1)} %get-tuple-element.22), channel_id=1, source_target_pairs={{0,1},{1,2},{2,3},{3,4},{4,5},{5,6},{6,7},{7,8},{8,9},{9,10},{10,1... | collective-permute-start | bytes 491528 | tf_op jit(solution)/shard_map/ppermute | solution.py:508
  17.4 12.4 %collective-permute-start.1 = (bf16[1,320,256]{2,1,0:T(8,128)(2,1)S(1)}, bf16[1,320,256]{2,1,0:T(8,128)(2,1)S(1)}, u32[]{:S(2)}, u32[]{:S(2)}) collective-permute-start(bf16[1,320,256]{2,1,0:T(8,128)(2,1)S(1)} %get-tuple-element.21), channel_id=1, source_target_pairs={{1,0},{2,1},{3,2},{4,3},{5,4},{6,5},{7,6},{8,7},{9,8},{10,9},{11,1... | collective-permute-start | bytes 491528 | tf_op jit(solution)/shard_map/ppermute | solution.py:509
  27.7 31.0 %copy-start.1 = (bf16[1,320,256]{2,1,0:T(8,128)(2,1)}, bf16[1,320,256]{2,1,0:T(8,128)(2,1)S(1)}, u32[]{:S(2)}) copy-start(bf16[1,320,256]{2,1,0:T(8,128)(2,1)S(1)} %collective-permute-done.above_ref.top_hbm) | copy-start | bytes 491524
  29.8 28.9 %copy-start.2 = (bf16[1,320,256]{2,1,0:T(8,128)(2,1)}, bf16[1,320,256]{2,1,0:T(8,128)(2,1)S(1)}, u32[]{:S(2)}) copy-start(bf16[1,320,256]{2,1,0:T(8,128)(2,1)S(1)} %collective-permute-done.1.below_ref.bot_hbm) | copy-start | bytes 491524
  47.5 13.7 %collective-permute-start.5 = (bf16[4,8,120,128]{3,2,1,0:T(8,128)(2,1)S(1)}, bf16[4,8,120,128]{3,2,1,0:T(8,128)(2,1)S(1)}, u32[]{:S(2)}, u32[]{:S(2)}) collective-permute-start(bf16[4,8,120,128]{3,2,1,0:T(8,128)(2,1)S(1)} %all_to_all.15.g_ref.own_ref), channel_id=1, source_target_pairs={{0,32},{32,0},{1,33},{33,1},{2,34},{34,2},{3,35},{35,3},{4,36},{36... | collective-permute-start | bytes 2949128 | tf_op jit(solution)/shard_map/ppermute | solution.py:503
  49.4 17.2 %collective-permute-start.2 = (bf16[8,120,128]{2,1,0:T(8,128)(2,1)S(1)}, bf16[8,120,128]{2,1,0:T(8,128)(2,1)S(1)}, u32[]{:S(2)}, u32[]{:S(2)}) collective-permute-start(bf16[8,120,128]{2,1,0:T(8,128)(2,1)S(1)} %get-tuple-element.13.own_ref), channel_id=1, source_target_pairs={{0,1},{1,2},{2,3},{3,0},{4,5},{5,6},{6,7},{7,4},{8,9},{9,10},{10,1... | collective-permute-start | bytes 737288 | tf_op jit(solution)/shard_map/ppermute | solution.py:537
  53.4 13.3 %collective-permute-start.3 = (bf16[8,120,128]{2,1,0:T(8,128)(2,1)S(1)}, bf16[8,120,128]{2,1,0:T(8,128)(2,1)S(1)}, u32[]{:S(2)}, u32[]{:S(2)}) collective-permute-start(bf16[8,120,128]{2,1,0:T(8,128)(2,1)S(1)} %get-tuple-element.13.own_ref), channel_id=1, source_target_pairs={{0,2},{1,3},{2,0},{3,1},{4,6},{5,7},{6,4},{7,5},{8,10},{9,11},{10,... | collective-permute-start | bytes 737288 | tf_op jit(solution)/shard_map/ppermute | solution.py:537
  55.7 14.4 %collective-permute-start.4 = (bf16[8,120,128]{2,1,0:T(8,128)(2,1)S(1)}, bf16[8,120,128]{2,1,0:T(8,128)(2,1)S(1)}, u32[]{:S(2)}, u32[]{:S(2)}) collective-permute-start(bf16[8,120,128]{2,1,0:T(8,128)(2,1)S(1)} %get-tuple-element.13.own_ref), channel_id=1, source_target_pairs={{0,3},{1,0},{2,1},{3,2},{4,7},{5,4},{6,5},{7,6},{8,11},{9,8},{10,9... | collective-permute-start | bytes 737288 | tf_op jit(solution)/shard_map/ppermute | solution.py:537
  61.2 27.1 %copy-start.6 = (f32[320]{0:T(512)S(1)}, f32[320]{0:T(512)}, u32[]{:S(2)}) copy-start(f32[320]{0:T(512)} %param.14) | copy-start | bytes 3844
  61.2 27.1 %copy-start.7 = (f32[320]{0:T(512)S(1)}, f32[320]{0:T(512)}, u32[]{:S(2)}) copy-start(f32[320]{0:T(512)} %param.15) | copy-start | bytes 3844
  61.2 27.1 %copy-start.8 = (f32[320]{0:T(512)S(1)}, f32[320]{0:T(512)}, u32[]{:S(2)}) copy-start(f32[320]{0:T(512)} %param.17) | copy-start | bytes 3844
  70.8 28.9 %collective-permute-start.6 = (bf16[32,120,128]{2,1,0:T(8,128)(2,1)S(1)}, bf16[32,120,128]{2,1,0:T(8,128)(2,1)S(1)}, u32[]{:S(2)}, u32[]{:S(2)}) collective-permute-start(bf16[32,120,128]{2,1,0:T(8,128)(2,1)S(1)} %join.1.own_ref), channel_id=1, source_target_pairs={{0,32},{32,0},{1,33},{33,1},{2,34},{34,2},{3,35},{35,3},{4,36},{36... | collective-permute-start | bytes 2949128 | tf_op jit(solution)/shard_map/ppermute | solution.py:503
  72.7 23.6 %collective-permute-start.7 = (bf16[1,320,256]{2,1,0:T(8,128)(2,1)}, bf16[1,320,256]{2,1,0:T(8,128)(2,1)}, u32[]{:S(2)}, u32[]{:S(2)}) collective-permute-start(bf16[1,320,256]{2,1,0:T(8,128)(2,1)} %get-tuple-element.18), channel_id=1, source_target_pairs={{0,1},{1,2},{2,3},{3,4},{4,5},{5,6},{6,7},{7,8},{8,9},{9,10},{10,1... | collective-permute-start | bytes 491528 | tf_op jit(solution)/shard_map/ppermute | solution.py:508
  74.6 21.6 %collective-permute-start.8 = (bf16[1,320,256]{2,1,0:T(8,128)(2,1)}, bf16[1,320,256]{2,1,0:T(8,128)(2,1)}, u32[]{:S(2)}, u32[]{:S(2)}) collective-permute-start(bf16[1,320,256]{2,1,0:T(8,128)(2,1)} %get-tuple-element.20), channel_id=1, source_target_pairs={{1,0},{2,1},{3,2},{4,3},{5,4},{6,5},{7,6},{8,7},{9,8},{10,9},{11,1... | collective-permute-start | bytes 491528 | tf_op jit(solution)/shard_map/ppermute | solution.py:509
  78.6 17.7 %all-to-all-start.2 = ((f32[32,1,128]{2,1,0:T(1,128)}), f32[32,1,128]{2,1,0:T(1,128)S(1)}, u32[]{:S(2)}, u32[]{:S(2)}) async-start(f32[32,1,128]{2,1,0:T(1,128)} %get-tuple-element.17.after_ref), calls=%async_computation.2 | async-start | bytes 32768 | tf_op jit(solution)/shard_map/all_to_all | solution.py:499

commit v3 on v2

--- a/solution.py
+++ b/solution.py
@@ -132,33 +132,43 @@
     return mean, jnp.sum(offs, axis=0, keepdims=True) + count * jnp.sum(d * d, axis=0, keepdims=True)
 
 
-def middle_kernel(g_ref, above_ref, below_ref, xch_ref, w2_ref, tail):
+def middle_kernel(g_ref, above_ref, below_ref, xch_hbm, w2_ref, tail, first, sems):
+    puts = [
+        pltpu.make_async_copy(g_ref.at[1:ZS, 0:CHUNK], xch_hbm.at[d, 1:ZS], sems.at[0, d]) for d in range(XS)
+    ]
+    for put in puts:
+        put.start()
     rows = pooled(*got_stats(g_ref[:, CHUNK - 8 : CHUNK, :].astype(f32)), LOCAL)
     tail[...] = g_ref[0, 0:CHUNK, :].astype(f32)
     put_stats(rows, tail)
-    first = tail[...].astype(bf16)
+    first[...] = tail[...].astype(bf16)
     for d in range(XS):
-        xch_ref[d, 0] = first
-        for z in range(1, ZS):
-            xch_ref[d, z] = g_ref[z, 0:CHUNK, :]
+        puts.append(pltpu.make_async_copy(first, xch_hbm.at[d, 0], sems.at[1, d]))
+        puts[-1].start()
     for z in range(ZS):
         w2_ref[z] = g_ref[z, CHUNK : 2 * CHUNK, :]
+    for put in puts:
+        put.wait()
 
 
 def middle(got, above, below):
     return pl.pallas_call(
         middle_kernel,
         out_shape=(
-            jax.ShapeDtypeStruct((XS, ZS, CHUNK, 128), bf16),
+            pltpu.HBM((XS, ZS, CHUNK, 128), bf16),
             pltpu.VMEM((ZS, CHUNK, 128), bf16),
         ),
         in_specs=[WHOLE, ANYWHERE, ANYWHERE],
-        out_specs=(WHOLE, WHOLE),
-        scratch_shapes=[pltpu.VMEM((CHUNK, 128), f32)],
+        out_specs=(FAR, WHOLE),
+        scratch_shapes=[
+            pltpu.VMEM((CHUNK, 128), f32),
+            pltpu.VMEM((CHUNK, 128), bf16),
+            pltpu.SemaphoreType.DMA((2, XS)),
+        ],
         compiler_params=PARAMS,
         cost_estimate=cost(1),
         name="middle",
-    )(got, above, below)
+    )(*near(got), above, below)
 
 
 def join_kernel(flags_ref, own_ref, a_ref, b_ref, c_ref, after_ref, out_ref):
@@ -284,12 +294,12 @@
 
 
 def norm2_kernel(
-    flags_ref, s_ref, top_ref, mid_hbm, bot_ref, gain_ref, beta_ref, act_ref, gains, betas, wide, here, sems
+    flags_ref, s_ref, top_hbm, mid_hbm, bot_hbm, gain_ref, beta_ref, act_ref, gains, betas, wide, here, sems
 ):
-    middle_row = fetched([mid_hbm.at[h] for h in range(4)], here, sems)
+    row = fetched([mid_hbm.at[h] for h in range(4)] + [top_hbm.at[0], bot_hbm.at[0]], here, sems)
     both = s_ref[:, 0, :]
     center, inv = combine(both[:, 0:GROUPS], both[:, GROUPS : 2 * GROUPS], LOCAL)
-    rows = lambda h: middle_row(h - 1) if 0 < h < 5 else (bot_ref if h else top_ref)[0]
+    rows = lambda h: row(h - 1 if 0 < h < 5 else 5 if h else 4)
     activate(flags_ref, rows, center, inv, gain_ref, beta_ref, (gains, betas), wide, act_ref)
 
 
@@ -323,13 +333,13 @@
     return pl.pallas_call(
         norm2_kernel,
         out_shape=ACT,
-        in_specs=[SCALARS, WHOLE, WHOLE, FAR, WHOLE, WHOLE, WHOLE],
+        in_specs=[SCALARS, WHOLE, FAR, FAR, FAR, WHOLE, WHOLE],
         out_specs=WHOLE,
-        scratch_shapes=NORM_SCRATCH + rows_here(4),
+        scratch_shapes=NORM_SCRATCH + rows_here(6),
         compiler_params=PARAMS,
         cost_estimate=cost(2),
         name="norm2",
-    )(flags, stats, top, far(mid), bot, gain.reshape(1, CU), beta.reshape(1, CU))
+    )(flags, stats, far(top), far(mid), far(bot), gain.reshape(1, CU), beta.reshape(1, CU))
 
 
 def shard_at(g_ref, d, rows):
@@ -369,18 +379,14 @@
 def rest_turned(w, wt):
     for p in range(3):
         part = jnp.concatenate([w[p * 3 * CU : (p + 1) * 3 * CU, :], jnp.zeros((ROWK - 3 * CU, 128), bf16)], axis=0)
-        wt[256:CU, p * ROWK : (p + 1) * ROWK] = jnp.transpose(part)[0:64, :]
-
-
-def rows_of(core):
-    return pl.ds(pl.multiple_of(core * 128, 128), 128)
-
-
-def conv_row(h, act_ref, wt):
-    return jnp.dot(wt[...], act_ref[h * ROWK : (h + 3) * ROWK, :], preferred_element_type=f32)
-
-
-def all_weights(flags_ref, own_ref, wto_ref, other_ref, many, many2, w, wt):
+        wt[128:192, p * ROWK : (p + 1) * ROWK] = jnp.transpose(part)[0:64, :]
+
+
+def conv(h, act_ref, w):
+    return jnp.dot(w[...], act_ref[h * ROWK : (h + 3) * ROWK, :], preferred_element_type=f32)
+
+
+def all_weights(flags_ref, own_ref, other_ref, many, many2, w, wt):
     core = flags_ref[0]
     for d in range(GROUPS):
         many2[d * 32 : (d + 1) * 32, :] = shard_at(own_ref, d, slice(CHUNK - 32, CHUNK))
@@ -393,21 +399,36 @@
     spread_out(other_ref, many)
     rest_of(1 - core, many, w)
     rest_turned(w, wt)
-    wt[rows_of(core), :] = wto_ref[...]
     for p, part in enumerate(block(many)):
-        wt[rows_of(1 - core), p * ROWK : (p + 1) * ROWK] = part
+        wt[0:128, p * ROWK : (p + 1) * ROWK] = part
+
+
+def convolve(flags_ref, own_ref, wto_ref, other_ref, act_ref, many, many2, w, wt, put):
+    core = flags_ref[0]
+    for h in range(4):
+        put(h, pl.multiple_of(core * 128, 128), 128, conv(h, act_ref, wto_ref))
+    all_weights(flags_ref, own_ref, other_ref, many, many2, w, wt)
+    for h in range(4):
+        both = conv(h, act_ref, wt)
+        put(h, pl.multiple_of((1 - core) * 128, 128), 128, both[0:128])
+        put(h, 256, 64, both[128:192])
 
 
 def conv1_kernel(
-    flags_ref, own_ref, wto_ref, other_ref, act_ref, shift_ref, hid_hbm, first_hbm, last_hbm, st_ref, many, many2, w, wt, full, hid, sems
+    flags_ref, own_ref, wto_ref, other_ref, act_ref, shift_ref, hid_hbm, first_hbm, last_hbm, st_ref, many, many2, w, wt, cols, full, hid, sems
 ):
-    all_weights(flags_ref, own_ref, wto_ref, other_ref, many, many2, w, wt)
-    shift = column_of(shift_ref[...])
-    shift = jnp.concatenate([shift, shift], axis=1)
-    for h in range(4):
-        row = (conv_row(h, act_ref, wt) + shift).astype(bf16)
-        hid[h] = row
-        widen(full, h * 2 * CU, row.astype(f32))
+    cols[...] = column_of(shift_ref[...])
+
+    def put(h, start, size, part):
+        add = cols[pl.ds(start, size), :]
+        row = (part + jnp.concatenate([add, add], axis=1)).astype(bf16)
+        hid[h, pl.ds(start, size), :] = row
+        for n in range(2):
+            at = start + (2 * h + n) * CU
+            at = at if isinstance(at, int) else pl.multiple_of(at, 64)
+            full[pl.ds(at, size), :] = row[:, n * 128 : (n + 1) * 128].astype(f32)
+
+    convolve(flags_ref, own_ref, wto_ref, other_ref, act_ref, many, many2, w, wt, put)
     puts = [
         pltpu.make_async_copy(hid.at[0:1], first_hbm, sems.at[0]),
         pltpu.make_async_copy(hid.at[3:4], last_hbm, sems.at[1]),
@@ -424,12 +445,13 @@
         put.wait()
 
 
-WT = (CU, 3 * ROWK)
+WT = (CU - 128, 3 * ROWK)
 CONV_SCRATCH = [
     MANY,
     pltpu.VMEM((GROUPS * 32, 128), f32),
     pltpu.VMEM((DEPTH, 128), bf16),
     pltpu.VMEM(WT, bf16),
+    pltpu.VMEM((CU, 128), f32),
 ]
 
 
@@ -474,12 +496,16 @@
     )(*near(own))
 
 
-def conv2_kernel(flags_ref, own_ref, wto_ref, other_ref, act_ref, bias_ref, x_ref, out_ref, many, many2, w, wt):
-    all_weights(flags_ref, own_ref, wto_ref, other_ref, many, many2, w, wt)
-    bias = column_of(bias_ref[...])
-    bias = jnp.concatenate([bias, bias], axis=1)
-    for h in range(4):
-        out_ref[h] = (x_ref[h].astype(f32) + (conv_row(h, act_ref, wt) + bias)).astype(bf16)
+def conv2_kernel(flags_ref, own_ref, wto_ref, other_ref, act_ref, bias_ref, x_ref, out_ref, many, many2, w, wt, cols):
+    cols[...] = column_of(bias_ref[...])
+
+    def put(h, start, size, part):
+        at = pl.ds(start, size)
+        add = cols[at, :]
+        total = x_ref[h, at, :].astype(f32) + (part + jnp.concatenate([add, add], axis=1))
+        out_ref[h, at, :] = total.astype(bf16)
+
+    convolve(flags_ref, own_ref, wto_ref, other_ref, act_ref, many, many2, w, wt, put)
 
 
 def conv2(flags, own, wto, other, act, bias, x):

time: 106 us -> 108 us (1.019)
  transfers between devices with their start and end apart: 11 -> 11, of which waited for: 5 -> 5; matrix products, arithmetic and copies ran while one was open for 0% -> 0% of each run, Pallas kernels for 11% -> 10%
where the time goes in v3:
time: 108 us; the launch traced here: 106 us
  starting transfers between devices  45.7 us (42%)
  waiting for transfers between devices  22.1 us (20%)
  Pallas kernels  20 us (19%)
  blocking collectives  17.4 us (16%)
    all_to_all x2, starting transfers between devices, to_all(): return lax.all_to_all(chunks, axis, 0, 0, tiled=True)  20.9 us
    all_to_all x1, blocking collectives, to_all(): return lax.all_to_all(chunks, axis, 0, 0, tiled=True)  17.4 us
    ppermute x3, starting transfers between devices, block_of(): lax.ppermute(w2z, 'row_1', [(i, (i + s) % XS) for i in range(XS)])  9.21 us
    ppermute x2, waiting for transfers between devices, edges(): above = lax.ppermute(last, ROW, [(i, i + 1) for i in range(count - 1)])  8.34 us
    all_to_all x2, waiting for transfers between devices, to_all(): return lax.all_to_all(chunks, axis, 0, 0, tiled=True)  7.91 us
    ppermute x2, starting transfers between devices, edges(): below = lax.ppermute(first, ROW, [(i + 1, i) for i in range(count - 1)])  5.93 us
    ppermute x2, starting transfers between devices, edges(): above = lax.ppermute(last, ROW, [(i, i + 1) for i in range(count - 1)])  5.76 us
    pallas_call x1, Pallas kernels, conv1(): pl.pallas_call(conv1_kernel, out_shape=(pltpu.HBM((4, CU, WIDTH), bf16),...  5.11 us
  transfers between devices with their start and end apart: 11, of which 5 were waited for; matrix products, arithmetic and copies ran while one was open for 0% of the time, Pallas kernels for 10%

profile of v3, /device:TPU:6, one launch (start us, length us, event | category | flops | bytes accessed | tf_op | source)
XLA Modules:
  0.0 105.7 jit_solution(3682911913222111312)
XLA Ops:
  0.1 3.1 %prep.1 = bf16[8,240,128]{2,1,0:T(8,128)(2,1)} custom-call(s32[4]{0:T(128)S(1)} %pad_add_fusion.flags_ref, bf16[4,320,256]{2,1,0:T(8,128)(2,1)} %bitcast.8, bf16[3,10,3,320]{3,2,1,0:T(4,128)(2,1)} %bitcast.12, bf16[3,10,3,320]{3,2,1,0:T(4,128)(2,1)} %bitcast.13), custom_call_target="tpu_custom_call" | custom-call | flops 600000000 | bytes 1048576 | tf_op jit(solution)/shard_map/prep/pallas_call | solution.py:216
  3.2 10.3 %all-to-all-start = ((bf16[8,240,128]{2,1,0:T(8,128)(2,1)}), bf16[8,240,128]{2,1,0:T(8,128)(2,1)S(1)}, u32[]{:S(2)}, u32[]{:S(2)}) async-start(bf16[8,240,128]{2,1,0:T(8,128)(2,1)} %prep.1), calls=%async_computation | async-start | bytes 983040 | tf_op jit(solution)/shard_map/all_to_all | solution.py:525
  13.5 3.8 %collective-permute-start = (bf16[1,320,256]{2,1,0:T(8,128)(2,1)S(1)}, bf16[1,320,256]{2,1,0:T(8,128)(2,1)S(1)}, u32[]{:S(2)}, u32[]{:S(2)}) collective-permute-start(bf16[1,320,256]{2,1,0:T(8,128)(2,1)S(1)} %get-tuple-element.22), channel_id=1, source_target_pairs={{0,1},{1,2},{2,3},{3,4},{4,5},{5,6},{6,7},{7,8},{8,9},{9,10},{10,1... | collective-permute-start | bytes 491528 | tf_op jit(solution)/shard_map/ppermute | solution.py:534
  17.4 2.0 %collective-permute-start.1 = (bf16[1,320,256]{2,1,0:T(8,128)(2,1)S(1)}, bf16[1,320,256]{2,1,0:T(8,128)(2,1)S(1)}, u32[]{:S(2)}, u32[]{:S(2)}) collective-permute-start(bf16[1,320,256]{2,1,0:T(8,128)(2,1)S(1)} %get-tuple-element.21), channel_id=1, source_target_pairs={{1,0},{2,1},{3,2},{4,3},{5,4},{6,5},{7,6},{8,7},{9,8},{10,9},{11,1... | collective-permute-start | bytes 491528 | tf_op jit(solution)/shard_map/ppermute | solution.py:535
  19.4 8.3 %collective-permute-done.above_ref.top_hbm = bf16[1,320,256]{2,1,0:T(8,128)(2,1)S(1)} collective-permute-done((bf16[1,320,256]{2,1,0:T(8,128)(2,1)S(1)}, bf16[1,320,256]{2,1,0:T(8,128)(2,1)S(1)}, u32[]{:S(2)}, u32[]{:S(2)}) %collective-permute-start) | collective-permute-done | bytes 163872 | tf_op jit(solution)/shard_map/ppermute | solution.py:534
  27.7 2.1 %collective-permute-done.1.below_ref.bot_hbm = bf16[1,320,256]{2,1,0:T(8,128)(2,1)S(1)} collective-permute-done((bf16[1,320,256]{2,1,0:T(8,128)(2,1)S(1)}, bf16[1,320,256]{2,1,0:T(8,128)(2,1)S(1)}, u32[]{:S(2)}, u32[]{:S(2)}) %collective-permute-start.1) | collective-permute-done | bytes 163872 | tf_op jit(solution)/shard_map/ppermute | solution.py:535
  30.2 1.0 middle.1
  31.2 17.4 %all_to_all.15.g_ref.own_ref = bf16[4,8,120,128]{3,2,1,0:T(8,128)(2,1)S(1)} all-to-all(bf16[4,8,120,128]{3,2,1,0:T(8,128)(2,1)} %get-tuple-element.14), channel_id=1, replica_groups=mesh['y'=8,'core'=2,'row_0'=8,'row_1'=4] {'row_1'}, dimensions={0} | all-to-all | bytes 1966080 | tf_op jit(solution)/shard_map/all_to_all | solution.py:525
  48.6 1.9 %collective-permute-start.5 = (bf16[4,8,120,128]{3,2,1,0:T(8,128)(2,1)S(1)}, bf16[4,8,120,128]{3,2,1,0:T(8,128)(2,1)S(1)}, u32[]{:S(2)}, u32[]{:S(2)}) collective-permute-start(bf16[4,8,120,128]{3,2,1,0:T(8,128)(2,1)S(1)} %all_to_all.15.g_ref.own_ref), channel_id=1, source_target_pairs={{0,32},{32,0},{1,33},{33,1},{2,34},{34,2},{3,35},{35,3},{4,36},{36... | collective-permute-start | bytes 2949128 | tf_op jit(solution)/shard_map/ppermute | solution.py:529
  50.5 4.0 %collective-permute-start.2 = (bf16[8,120,128]{2,1,0:T(8,128)(2,1)S(1)}, bf16[8,120,128]{2,1,0:T(8,128)(2,1)S(1)}, u32[]{:S(2)}, u32[]{:S(2)}) collective-permute-start(bf16[8,120,128]{2,1,0:T(8,128)(2,1)S(1)} %get-tuple-element.13.own_ref), channel_id=1, source_target_pairs={{0,1},{1,2},{2,3},{3,0},{4,5},{5,6},{6,7},{7,4},{8,9},{9,10},{10,1... | collective-permute-start | bytes 737288 | tf_op jit(solution)/shard_map/ppermute | solution.py:563
  54.5 2.3 %collective-permute-start.3 = (bf16[8,120,128]{2,1,0:T(8,128)(2,1)S(1)}, bf16[8,120,128]{2,1,0:T(8,128)(2,1)S(1)}, u32[]{:S(2)}, u32[]{:S(2)}) collective-permute-start(bf16[8,120,128]{2,1,0:T(8,128)(2,1)S(1)} %get-tuple-element.13.own_ref), channel_id=1, source_target_pairs={{0,2},{1,3},{2,0},{3,1},{4,6},{5,7},{6,4},{7,5},{8,10},{9,11},{10,... | collective-permute-start | bytes 737288 | tf_op jit(solution)/shard_map/ppermute | solution.py:563
  56.8 2.9 %collective-permute-start.4 = (bf16[8,120,128]{2,1,0:T(8,128)(2,1)S(1)}, bf16[8,120,128]{2,1,0:T(8,128)(2,1)S(1)}, u32[]{:S(2)}, u32[]{:S(2)}) collective-permute-start(bf16[8,120,128]{2,1,0:T(8,128)(2,1)S(1)} %get-tuple-element.13.own_ref), channel_id=1, source_target_pairs={{0,3},{1,0},{2,1},{3,2},{4,7},{5,4},{6,5},{7,6},{8,11},{9,8},{10,9... | collective-permute-start | bytes 737288 | tf_op jit(solution)/shard_map/ppermute | solution.py:563
  59.9 2.4 %norm1.1 = (bf16[6144,256]{1,0:T(8,128)(2,1)S(1)}, bf16[128,3072]{1,0:T(8,128)(2,1)S(1)}) custom-call(s32[4]{0:T(128)S(1)} %pad_add_fusion.flags_ref, bf16[4,8,120,128]{3,2,1,0:T(8,128)(2,1)S(1)} %all_to_all.15.g_ref.own_ref, bf16[1,320,256]{2,1,0:T(8,128)(2,1)} %copy-done.1, bf16[4,320,256]{2,1,0:T(8,128)(2,1)S(1)} %bitcast.10, ...), custom_call_target="tpu_custom_call" | custom-call | flops 600000000 | bytes 1048576 | tf_op jit(solution)/shard_map/norm1/pallas_call | solution.py:320
  62.3 5.1 %conv1.1 = (bf16[4,320,256]{2,1,0:T(8,128)(2,1)}, bf16[1,320,256]{2,1,0:T(8,128)(2,1)}, bf16[1,320,256]{2,1,0:T(8,128)(2,1)}, f32[32,1,128]{2,1,0:T(1,128)}) custom-call(s32[4]{0:T(128)S(1)} %pad_add_fusion.flags_ref, bf16[4,8,120,128]{3,2,1,0:T(8,128)(2,1)S(1)} %all_to_all.15.g_ref.own_ref, bf16[128,3072]{1,0:T(8,128)(2,1)S(1)} %get-tuple-element.15.wto_ref, ...), custom_call_target="tpu_custom_call" | custom-call | flops 1000000000 | bytes 1048576 | tf_op jit(solution)/shard_map/conv1/pallas_call | solution.py:460
  67.5 3.8 %collective-permute-done.4.c_ref = bf16[8,120,128]{2,1,0:T(8,128)(2,1)S(1)} collective-permute-done((bf16[8,120,128]{2,1,0:T(8,128)(2,1)S(1)}, bf16[8,120,128]{2,1,0:T(8,128)(2,1)S(1)}, u32[]{:S(2)}, u32[]{:S(2)}) %collective-permute-start.4) | collective-permute-done | bytes 245792 | tf_op jit(solution)/shard_map/ppermute | solution.py:563
  71.3 0.6 join.1.own_ref
  71.9 1.9 %collective-permute-start.6 = (bf16[32,120,128]{2,1,0:T(8,128)(2,1)S(1)}, bf16[32,120,128]{2,1,0:T(8,128)(2,1)S(1)}, u32[]{:S(2)}, u32[]{:S(2)}) collective-permute-start(bf16[32,120,128]{2,1,0:T(8,128)(2,1)S(1)} %join.1.own_ref), channel_id=1, source_target_pairs={{0,32},{32,0},{1,33},{33,1},{2,34},{34,2},{3,35},{35,3},{4,36},{36... | collective-permute-start | bytes 2949128 | tf_op jit(solution)/shard_map/ppermute | solution.py:529
  73.8 1.9 %collective-permute-start.7 = (bf16[1,320,256]{2,1,0:T(8,128)(2,1)}, bf16[1,320,256]{2,1,0:T(8,128)(2,1)}, u32[]{:S(2)}, u32[]{:S(2)}) collective-permute-start(bf16[1,320,256]{2,1,0:T(8,128)(2,1)} %get-tuple-element.18), channel_id=1, source_target_pairs={{0,1},{1,2},{2,3},{3,4},{4,5},{5,6},{6,7},{7,8},{8,9},{9,10},{10,1... | collective-permute-start | bytes 491528 | tf_op jit(solution)/shard_map/ppermute | solution.py:534
  75.8 3.9 %collective-permute-start.8 = (bf16[1,320,256]{2,1,0:T(8,128)(2,1)}, bf16[1,320,256]{2,1,0:T(8,128)(2,1)}, u32[]{:S(2)}, u32[]{:S(2)}) collective-permute-start(bf16[1,320,256]{2,1,0:T(8,128)(2,1)} %get-tuple-element.20), channel_id=1, source_target_pairs={{1,0},{2,1},{3,2},{4,3},{5,4},{6,5},{7,6},{8,7},{9,8},{10,9},{11,1... | collective-permute-start | bytes 491528 | tf_op jit(solution)/shard_map/ppermute | solution.py:535
  79.7 10.6 %all-to-all-start.2 = ((f32[32,1,128]{2,1,0:T(1,128)}), f32[32,1,128]{2,1,0:T(1,128)S(1)}, u32[]{:S(2)}, u32[]{:S(2)}) async-start(f32[32,1,128]{2,1,0:T(1,128)} %get-tuple-element.17.after_ref), calls=%async_computation.2 | async-start | bytes 32768 | tf_op jit(solution)/shard_map/all_to_all | solution.py:525
  90.4 0.4 own2.1.wto_ref
  90.7 7.6 %all-to-all-done.2.s_ref = f32[32,1,128]{2,1,0:T(1,128)S(1)} async-done(((f32[32,1,128]{2,1,0:T(1,128)}), f32[32,1,128]{2,1,0:T(1,128)S(1)}, u32[]{:S(2)}, u32[]{:S(2)}) %all-to-all-start.2) | async-done | bytes 16416 | tf_op jit(solution)/shard_map/all_to_all | solution.py:525
  98.3 3.1 %norm2.1.act_ref = bf16[6144,256]{1,0:T(8,128)(2,1)S(1)} custom-call(s32[4]{0:T(128)S(1)} %pad_add_fusion.flags_ref, f32[32,1,128]{2,1,0:T(1,128)S(1)} %all-to-all-done.2.s_ref, bf16[1,320,256]{2,1,0:T(8,128)(2,1)} %collective-permute-done.7.top_hbm, bf16[4,320,256]{2,1,0:T(8,128)(2,1)} %get-tuple-element.19.mid_hbm, ...), custom_call_target="tpu_custom_call" | custom-call | flops 400000000 | bytes 1048576 | tf_op jit(solution)/shard_map/norm2/pallas_call | solution.py:333
  101.4 4.3 %conv2.1 = bf16[4,320,256]{2,1,0:T(8,128)(2,1)} custom-call(s32[4]{0:T(128)S(1)} %pad_add_fusion.flags_ref, bf16[32,120,128]{2,1,0:T(8,128)(2,1)S(1)} %join.1.own_ref, bf16[128,3072]{1,0:T(8,128)(2,1)S(1)} %own2.1.wto_ref, bf16[32,120,128]{2,1,0:T(8,128)(2,1)S(1)} %collective-permute-done.6.other_ref, bf16[6144,256]{1,0:T(8,128)(2,1)S(1)} %norm2.1.act_ref, ...), custom_call_target="tpu_custom_call" | custom-call | flops 800000000 | bytes 1048576 | tf_op jit(solution)/shard_map/conv2/pallas_call | solution.py:512
  (33 shorter events, 0.5 us)
Async XLA Ops:
  0.0 13.5 %copy-start = (bf16[4,256,320]{1,2,0:T(8,128)(2,1)S(1)}, bf16[4,256,320]{1,2,0:T(8,128)(2,1)}, u32[]{:S(2)}) copy-start(bf16[4,256,320]{1,2,0:T(8,128)(2,1)} %param.9) | copy-start | bytes 1966084
  0.1 59.7 %copy-start.3 = (f32[320]{0:T(512)S(1)}, f32[320]{0:T(512)}, u32[]{:S(2)}) copy-start(f32[320]{0:T(512)} %param.10) | copy-start | bytes 3844
  0.1 59.7 %copy-start.4 = (f32[320]{0:T(512)S(1)}, f32[320]{0:T(512)}, u32[]{:S(2)}) copy-start(f32[320]{0:T(512)} %param.11) | copy-start | bytes 3844
  0.1 59.7 %copy-start.5 = (f32[320]{0:T(512)S(1)}, f32[320]{0:T(512)}, u32[]{:S(2)}) copy-start(f32[320]{0:T(512)} %param.13) | copy-start | bytes 3844
  3.2 27.0 %all-to-all-start = ((bf16[8,240,128]{2,1,0:T(8,128)(2,1)}), bf16[8,240,128]{2,1,0:T(8,128)(2,1)S(1)}, u32[]{:S(2)}, u32[]{:S(2)}) async-start(bf16[8,240,128]{2,1,0:T(8,128)(2,1)} %prep.1), calls=%async_computation | async-start | bytes 983040 | tf_op jit(solution)/shard_map/all_to_all | solution.py:525
  13.5 14.2 %collective-permute-start = (bf16[1,320,256]{2,1,0:T(8,128)(2,1)S(1)}, bf16[1,320,256]{2,1,0:T(8,128)(2,1)S(1)}, u32[]{:S(2)}, u32[]{:S(2)}) collective-permute-start(bf16[1,320,256]{2,1,0:T(8,128)(2,1)S(1)} %get-tuple-element.22), channel_id=1, source_target_pairs={{0,1},{1,2},{2,3},{3,4},{4,5},{5,6},{6,7},{7,8},{8,9},{9,10},{10,1... | collective-permute-start | bytes 491528 | tf_op jit(solution)/shard_map/ppermute | solution.py:534
  17.4 12.4 %collective-permute-start.1 = (bf16[1,320,256]{2,1,0:T(8,128)(2,1)S(1)}, bf16[1,320,256]{2,1,0:T(8,128)(2,1)S(1)}, u32[]{:S(2)}, u32[]{:S(2)}) collective-permute-start(bf16[1,320,256]{2,1,0:T(8,128)(2,1)S(1)} %get-tuple-element.21), channel_id=1, source_target_pairs={{1,0},{2,1},{3,2},{4,3},{5,4},{6,5},{7,6},{8,7},{9,8},{10,9},{11,1... | collective-permute-start | bytes 491528 | tf_op jit(solution)/shard_map/ppermute | solution.py:535
  27.7 32.1 %copy-start.1 = (bf16[1,320,256]{2,1,0:T(8,128)(2,1)}, bf16[1,320,256]{2,1,0:T(8,128)(2,1)S(1)}, u32[]{:S(2)}) copy-start(bf16[1,320,256]{2,1,0:T(8,128)(2,1)S(1)} %collective-permute-done.above_ref.top_hbm) | copy-start | bytes 491524
  29.8 30.0 %copy-start.2 = (bf16[1,320,256]{2,1,0:T(8,128)(2,1)}, bf16[1,320,256]{2,1,0:T(8,128)(2,1)S(1)}, u32[]{:S(2)}) copy-start(bf16[1,320,256]{2,1,0:T(8,128)(2,1)S(1)} %collective-permute-done.1.below_ref.bot_hbm) | copy-start | bytes 491524
  48.6 13.7 %collective-permute-start.5 = (bf16[4,8,120,128]{3,2,1,0:T(8,128)(2,1)S(1)}, bf16[4,8,120,128]{3,2,1,0:T(8,128)(2,1)S(1)}, u32[]{:S(2)}, u32[]{:S(2)}) collective-permute-start(bf16[4,8,120,128]{3,2,1,0:T(8,128)(2,1)S(1)} %all_to_all.15.g_ref.own_ref), channel_id=1, source_target_pairs={{0,32},{32,0},{1,33},{33,1},{2,34},{34,2},{3,35},{35,3},{4,36},{36... | collective-permute-start | bytes 2949128 | tf_op jit(solution)/shard_map/ppermute | solution.py:529
  50.5 16.9 %collective-permute-start.2 = (bf16[8,120,128]{2,1,0:T(8,128)(2,1)S(1)}, bf16[8,120,128]{2,1,0:T(8,128)(2,1)S(1)}, u32[]{:S(2)}, u32[]{:S(2)}) collective-permute-start(bf16[8,120,128]{2,1,0:T(8,128)(2,1)S(1)} %get-tuple-element.13.own_ref), channel_id=1, source_target_pairs={{0,1},{1,2},{2,3},{3,0},{4,5},{5,6},{6,7},{7,4},{8,9},{9,10},{10,1... | collective-permute-start | bytes 737288 | tf_op jit(solution)/shard_map/ppermute | solution.py:563
  54.5 12.9 %collective-permute-start.3 = (bf16[8,120,128]{2,1,0:T(8,128)(2,1)S(1)}, bf16[8,120,128]{2,1,0:T(8,128)(2,1)S(1)}, u32[]{:S(2)}, u32[]{:S(2)}) collective-permute-start(bf16[8,120,128]{2,1,0:T(8,128)(2,1)S(1)} %get-tuple-element.13.own_ref), channel_id=1, source_target_pairs={{0,2},{1,3},{2,0},{3,1},{4,6},{5,7},{6,4},{7,5},{8,10},{9,11},{10,... | collective-permute-start | bytes 737288 | tf_op jit(solution)/shard_map/ppermute | solution.py:563
  56.8 14.4 %collective-permute-start.4 = (bf16[8,120,128]{2,1,0:T(8,128)(2,1)S(1)}, bf16[8,120,128]{2,1,0:T(8,128)(2,1)S(1)}, u32[]{:S(2)}, u32[]{:S(2)}) collective-permute-start(bf16[8,120,128]{2,1,0:T(8,128)(2,1)S(1)} %get-tuple-element.13.own_ref), channel_id=1, source_target_pairs={{0,3},{1,0},{2,1},{3,2},{4,7},{5,4},{6,5},{7,6},{8,11},{9,8},{10,9... | collective-permute-start | bytes 737288 | tf_op jit(solution)/shard_map/ppermute | solution.py:563
  62.3 28.0 %copy-start.6 = (f32[320]{0:T(512)S(1)}, f32[320]{0:T(512)}, u32[]{:S(2)}) copy-start(f32[320]{0:T(512)} %param.14) | copy-start | bytes 3844
  62.3 28.0 %copy-start.7 = (f32[320]{0:T(512)S(1)}, f32[320]{0:T(512)}, u32[]{:S(2)}) copy-start(f32[320]{0:T(512)} %param.15) | copy-start | bytes 3844
  62.3 28.0 %copy-start.8 = (f32[320]{0:T(512)S(1)}, f32[320]{0:T(512)}, u32[]{:S(2)}) copy-start(f32[320]{0:T(512)} %param.17) | copy-start | bytes 3844
  71.9 29.5 %collective-permute-start.6 = (bf16[32,120,128]{2,1,0:T(8,128)(2,1)S(1)}, bf16[32,120,128]{2,1,0:T(8,128)(2,1)S(1)}, u32[]{:S(2)}, u32[]{:S(2)}) collective-permute-start(bf16[32,120,128]{2,1,0:T(8,128)(2,1)S(1)} %join.1.own_ref), channel_id=1, source_target_pairs={{0,32},{32,0},{1,33},{33,1},{2,34},{34,2},{3,35},{35,3},{4,36},{36... | collective-permute-start | bytes 2949128 | tf_op jit(solution)/shard_map/ppermute | solution.py:529
  73.8 24.5 %collective-permute-start.7 = (bf16[1,320,256]{2,1,0:T(8,128)(2,1)}, bf16[1,320,256]{2,1,0:T(8,128)(2,1)}, u32[]{:S(2)}, u32[]{:S(2)}) collective-permute-start(bf16[1,320,256]{2,1,0:T(8,128)(2,1)} %get-tuple-element.18), channel_id=1, source_target_pairs={{0,1},{1,2},{2,3},{3,4},{4,5},{5,6},{6,7},{7,8},{8,9},{9,10},{10,1... | collective-permute-start | bytes 491528 | tf_op jit(solution)/shard_map/ppermute | solution.py:534
  75.8 22.5 %collective-permute-start.8 = (bf16[1,320,256]{2,1,0:T(8,128)(2,1)}, bf16[1,320,256]{2,1,0:T(8,128)(2,1)}, u32[]{:S(2)}, u32[]{:S(2)}) collective-permute-start(bf16[1,320,256]{2,1,0:T(8,128)(2,1)} %get-tuple-element.20), channel_id=1, source_target_pairs={{1,0},{2,1},{3,2},{4,3},{5,4},{6,5},{7,6},{8,7},{9,8},{10,9},{11,1... | collective-permute-start | bytes 491528 | tf_op jit(solution)/shard_map/ppermute | solution.py:535
  79.7 18.6 %all-to-all-start.2 = ((f32[32,1,128]{2,1,0:T(1,128)}), f32[32,1,128]{2,1,0:T(1,128)S(1)}, u32[]{:S(2)}, u32[]{:S(2)}) async-start(f32[32,1,128]{2,1,0:T(1,128)} %get-tuple-element.17.after_ref), calls=%async_computation.2 | async-start | bytes 32768 | tf_op jit(solution)/shard_map/all_to_all | solution.py:525
